TPU v7x, 256 devices: a whole 4x4x8 slice. The times are simulated.
256 devices in a mesh: pa: 16 (over x_hi, z), gz: 16 (over x_lo, y, core).
Axes of the slice: x: 4 (x_hi: 2, x_lo: 2; x = x_hi * 2 + x_lo), y: 4, z: 8, core: 2. Of those that a mesh axis runs over, the one named last changes fastest.
Arguments:
- source: float32 [128, 768, 768], P('gz', 'pa'), may hold values from -24 to 24
- cell_width: float32 [128], P('gz'), may hold values from 0.5 to 2
Outputs:
- potential: float32 [128, 768, 768], P('gz', 'pa')
All inputs are finite; a program needn't handle non-finite values.
Results may differ from a plain program's by a relative error of at most 0.00085.
Values sent between devices are 32-bit elements; how exact they have to be, the bound alone decides.
A program may use at most 64 MiB of HBM per device.

v0:
```python
import functools

import jax
import jax.numpy as jnp
import numpy as np
from jax import lax
from jax.experimental import pallas as pl
from jax.experimental.pallas import tpu as pltpu
from jax.sharding import PartitionSpec as P

F32 = jnp.float32
BF16 = jnp.bfloat16
N = 768
NB = 16
ZL = 8
YL = 48
LANES = 128
CH = N // LANES
SOLVERS = tuple(g for g in range(NB) if g not in (0, 4, 10, 14))
NS = len(SOLVERS)
HALF = N // 2


def split64(x):
    hi = x.astype(np.float32).astype(jnp.bfloat16)
    lo = (x - hi.astype(np.float64)).astype(np.float32).astype(jnp.bfloat16)
    return np.stack([hi, lo])


@functools.cache
def tables():
    n = np.arange(N)
    phases = n[:, None] * (2 * n[None, :] + 1) % (4 * N)
    weights = np.where(n == 0, np.sqrt(1.0 / N), np.sqrt(2.0 / N))
    cos_t = weights[:, None] * np.cos(phases * (np.pi / (2 * N)))

    def sine(width, rows, cols):
        p = rows[:, None] * cols[None, :] % (2 * (width + 1))
        return np.sqrt(2.0 / (width + 1)) * np.sin(p * (np.pi / (width + 1)))

    m = n + 1
    sin_t = sine(N, m, m)
    ml = np.arange(1, YL + 1)
    s48 = sine(YL, ml, ml)
    hi, lo = split64(s48)
    s48st = np.concatenate([hi, hi, lo], axis=1)
    mc = np.zeros((ZL * YL, LANES))
    mc[:YL, :YL] = s48
    mc[(ZL - 1) * YL :, YL : 2 * YL] = s48
    for z in range(ZL):
        mc[z * YL : (z + 1) * YL, 2 * YL + 2 * z] = s48[:, 0]
        mc[z * YL : (z + 1) * YL, 2 * YL + 2 * z + 1] = s48[:, YL - 1]
    own = np.zeros((NB, ZL, 2, N))
    beside = np.zeros((NB, ZL, 2, N))
    for p in range(NB):
        for e in range(2):
            row = YL * p + (YL - 1) * e
            own[p, :, e] = sin_t[row]
            near = row + (1 if e else -1)
            if 0 <= near < N:
                beside[p, :, e] = sin_t[near]
    own = own.reshape(2 * ZL * NB, N)
    beside = beside.reshape(2 * ZL * NB, N)
    lam_k = 4 * np.sin(n * np.pi / (2 * N)) ** 2
    lam_l = 4 * np.sin(m * np.pi / (2 * (N + 1))) ** 2
    lam_s = 4 * np.sin(ml * np.pi / (2 * (YL + 1))) ** 2
    rows = np.zeros((8, N), np.float32)
    rows[0] = lam_k
    rows[1] = lam_l
    return dict(
        cos=split64(cos_t),
        sin=split64(sin_t),
        s48=s48st,
        mct=split64(mc.T.copy()),
        mc=split64(mc),
        win=split64(own),
        wout=split64(beside.T.copy()),
        rows=rows,
        lam_s=np.broadcast_to(lam_s[:, None], (YL, LANES)).astype(np.float32),
        lam_k=np.broadcast_to(lam_k[:, None], (N, LANES)).astype(np.float32),
    )


TABLES = ("cos", "sin", "s48", "mct", "mc", "win", "wout", "rows", "lam_s", "lam_k")


def cut(x):
    hi = x.astype(BF16)
    return hi, (x - hi.astype(F32)).astype(BF16)


def dot(a, b):
    return jnp.dot(a, b, preferred_element_type=F32)


def dot_nt(a, b):
    return lax.dot_general(a, b, (((1,), (1,)), ((), ())), preferred_element_type=F32)


def by_table(x, hi, lo, f=dot):
    a, b = cut(x)
    return f(a, hi) + f(b, hi) + f(a, lo)


def table_by(hi, lo, x):
    a, b = cut(x)
    return dot(hi, a) + dot(hi, b) + dot(lo, a)


def recip(x):
    return 1.0 / x


def lane_iota(rows):
    return lax.broadcasted_iota(jnp.int32, (rows, LANES), 1)


def remote(src, dst, send, recv, where):
    return pltpu.make_async_remote_copy(
        src_ref=src,
        dst_ref=dst,
        send_sem=send,
        recv_sem=recv,
        device_id=where,
        device_id_type=pl.DeviceIdType.MESH,
    )


def rolled(x, shift):
    shift %= LANES
    return x if shift == 0 else pltpu.roll(x, shift, axis=1)


def kernel(
    src, cw, cos_r, sin_r, s48, mct, mc, win, wout, lam_rows, lam_s, lam_k, out,
    s_hi, s_lo, fh, work, eloc, pbuf, precv, wmine, widths, alpha, beta, planes, rhy, eg,
    qbuf, qrecv, rbuf, rrecv, c00, c70, c70c, ci, cia, cc, hh, bbuf, brecv, scale,
    psend_s, precv_s, wsend_s, wrecv_s, qsend_s, qrecv_s, rsend_s, rrecv_s, bsend_s, brecv_s,
):
    pa = lax.axis_index("pa")
    gz = lax.axis_index("gz")

    def peer(me, d):
        return lax.rem(me + d, NB)

    barrier = pltpu.get_barrier_semaphore()
    for d in range(1, NB):
        pl.semaphore_signal(barrier, inc=1, device_id={"pa": peer(pa, d)}, device_id_type=pl.DeviceIdType.MESH)
        pl.semaphore_signal(barrier, inc=1, device_id={"gz": peer(gz, d)}, device_id_type=pl.DeviceIdType.MESH)

    for z in range(ZL):
        wmine[z : z + 1, :] = jnp.full((1, LANES), cw[z], F32)
    x = src[...]
    a, b = cut(x)
    s_hi[...] = a
    s_lo[...] = b

    def forward(c):
        cols = slice(c * 256, (c + 1) * 256)
        hi = cos_r[0, cols, :]
        lo = cos_r[1, cols, :]
        f = dot_nt(s_hi[...], hi) + dot_nt(s_lo[...], hi) + dot_nt(s_hi[...], lo)
        for z in range(ZL):
            a, b = cut(f[z * YL : (z + 1) * YL])
            fh[z, :, cols] = dot(s48[...], jnp.concatenate([a, b, a], axis=0))

    forward(0)
    pl.semaphore_wait(barrier, 2 * (NB - 1))
    wcopies = [
        remote(wmine, widths.at[gz], wsend_s.at[d], wrecv_s.at[gz], {"gz": peer(gz, d)})
        for d in range(1, NB)
    ]
    for copy in wcopies:
        copy.start()
    widths[gz] = wmine[...]
    forward(1)
    forward(2)
    for copy in wcopies:
        copy.wait_send()
    for d in range(1, NB):
        g = peer(gz, d)
        remote(wmine, widths.at[g], wsend_s.at[d], wrecv_s.at[g], {"gz": g}).wait_recv()

    w = widths[...].reshape(NB * ZL, LANES)
    at = lax.broadcasted_iota(jnp.int32, (NB * ZL, LANES), 0)
    before = jnp.where(at == 0, 0.0, pltpu.roll(w, 1, axis=0))
    after = jnp.where(at == NB * ZL - 1, 0.0, pltpu.roll(w, NB * ZL - 1, axis=0))
    alpha[...] = 2.0 / ((before + w) * w)
    beta[...] = 2.0 / ((w + after) * w)
    mine = pl.ds(pl.multiple_of(gz * ZL, ZL), ZL)
    al_b = alpha[mine, :]
    be_b = beta[mine, :]

    def a_of(z, like):
        return jnp.broadcast_to(al_b[z : z + 1, :], like)

    def b_of(z, like):
        return jnp.broadcast_to(be_b[z : z + 1, :], like)

    tile = (YL, LANES)

    def factor(e_ref, cols, lam):
        e = None
        for z in range(ZL):
            d = a_of(z, tile) + b_of(z, tile) + lam
            if z:
                d = d - a_of(z, tile) * b_of(z - 1, tile) * e
            e = recip(d)
            e_ref[z, :, cols] = e

    def solve(rhs_of, e_ref, cols, x_ref):
        y = None
        for z in range(ZL):
            r = rhs_of(z)
            if z:
                r = r + a_of(z, tile) * y
            y = e_ref[z, :, cols] * r
            x_ref[z, :, cols] = y
        first = y
        last = y
        for z in range(ZL - 2, -1, -1):
            first = x_ref[z, :, cols] + e_ref[z, :, cols] * b_of(z, tile) * first
            x_ref[z, :, cols] = first
        return first, last

    def block(c):
        cols = pl.ds(pl.multiple_of(c * LANES, LANES), LANES)
        lam = lam_s[...] + lam_rows[0:1, cols]
        factor(eloc, cols, lam)
        solve(lambda z: fh[z, :, cols], eloc, cols, work)
        v = work[:, :, cols].reshape(ZL * YL, LANES)
        p = table_by(mct[0], mct[1], v)
        pbuf[cols, :] = jnp.transpose(p)

    pl.loop(0, CH)(block)

    def mine48(ref, q):
        return ref.at[pl.ds(pl.multiple_of(q * YL, YL), YL), :]

    pcopies = [
        remote(mine48(pbuf, peer(pa, d)), precv.at[pa], psend_s.at[d], precv_s.at[pa], {"pa": peer(pa, d)})
        for d in range(1, NB)
    ]
    for copy in pcopies:
        copy.start()
    precv[pa] = pbuf[pl.ds(pl.multiple_of(pa * YL, YL), YL), :]

    lk = lam_k[pl.ds(pl.multiple_of(pa * YL, YL), YL), :]

    def global_factor(c):
        cols = pl.ds(pl.multiple_of(c * LANES, LANES), LANES)
        factor(eg, cols, lk + lam_rows[1:2, cols])

    pl.loop(0, CH)(global_factor)

    idle_before = sum(((gz > g).astype(jnp.int32) for g in (0, 4, 10, 14)), jnp.int32(0))
    me_s = gz - idle_before
    is_solver = (gz != 0) & (gz != 4) & (gz != 10) & (gz != 14)
    krow = lam_k[pl.ds(pl.multiple_of(pa * YL + 8 * lax.div(me_s, 2), 8), 8), :]
    half = lax.rem(me_s, 2)

    def row_of(ref, i):
        v = ref[pl.ds(i, 1), :]
        return jnp.broadcast_to(jnp.concatenate([v, v, v], axis=1), (8, HALF))

    @pl.when(is_solver)
    def _():
        lam = jnp.concatenate([krow, krow, krow], axis=1) + lam_rows[
            1:2, pl.ds(pl.multiple_of(half * HALF, HALF), HALF)
        ]

        def coefficients(b, carry):
            al = [row_of(alpha, b * ZL + z) for z in range(ZL)]
            be = [row_of(beta, b * ZL + z) for z in range(ZL)]
            e = recip(al[0] + be[0] + lam)
            prod_e = e
            prod_a = al[0]
            prod_b = be[0]
            for z in range(1, ZL):
                e = recip(al[z] + be[z] + lam - al[z] * be[z - 1] * e)
                prod_e = prod_e * e * al[z]
                prod_b = prod_b * be[z] / al[z]
            a70 = prod_e * prod_a
            a07 = prod_e * prod_b
            a77 = e * be[ZL - 1]
            g = recip(al[ZL - 1] + be[ZL - 1] + lam)
            for z in range(ZL - 2, -1, -1):
                g = recip(al[z] + be[z] + lam - be[z] * al[z + 1] * g)
            a00 = g * al[0]
            c00[b] = a00
            c70[b] = a70
            cia[b] = a07
            cc[b] = a77
            return carry

        lax.fori_loop(0, NB, coefficients, 0)
        c = jnp.zeros((8, HALF), F32)
        for b in range(NB):
            inv = recip(1.0 - c00[b] * c)
            ia = inv * cia[b]
            bc = c70[b] * c
            ci[b] = inv
            cia[b] = ia
            c70c[b] = bc
            c = cc[b] + bc * ia
            cc[b] = c

    for copy in pcopies:
        copy.wait_send()
    for d in range(1, NB):
        p = peer(pa, d)
        remote(mine48(pbuf, p), precv.at[p], psend_s.at[d], precv_s.at[p], {"pa": p}).wait_recv()

    lanes = lane_iota(YL)
    zero = jnp.zeros(tile, F32)

    def gathered(base, t):
        value = zero
        for p in range(NB):
            start = YL * p - LANES * t
            if start + YL <= 0 or start >= LANES:
                continue
            piece = rolled(precv[p], start - base)
            value = jnp.where((lanes >= start) & (lanes < start + YL), piece, value)
        return value

    for t in range(CH):
        planes[0:YL, t * LANES : (t + 1) * LANES] = gathered(0, t)
        planes[YL : 2 * YL, t * LANES : (t + 1) * LANES] = gathered(YL, t)

    def beside(t):
        value = zero
        odd = lax.rem(lanes, 2) == 1
        for p in range(8 * t, 8 * t + 8):
            at_p = (lanes >= 16 * (p - 8 * t)) & (lanes < 16 * (p - 8 * t) + 16)
            start = 16 * (p - 8 * t) - 2 * YL
            if p > 0:
                value = jnp.where(at_p & ~odd, rolled(precv[p - 1], start - 1), value)
            if p < NB - 1:
                value = jnp.where(at_p & odd, rolled(precv[p + 1], start + 1), value)
        return value

    near = [beside(t) for t in range(2)]
    at_z = [lax.div(lax.rem(lanes, 16), 2) == z for z in range(ZL)]
    for z in range(ZL):
        a, b = cut(jnp.concatenate([jnp.where(at_z[z], v, 0.0) for v in near], axis=1))
        s_hi[z * YL : (z + 1) * YL, 0:256] = a
        s_lo[z * YL : (z + 1) * YL, 0:256] = b

    for n in range(3):
        cols = slice(n * 256, (n + 1) * 256)
        r = dot(s_hi[:, 0:256], win[0, :, cols])
        r = r + dot(s_lo[:, 0:256], win[0, :, cols]) + dot(s_hi[:, 0:256], win[1, :, cols])
        rhy[:, :, cols] = r.reshape(ZL, YL, 256)
    ph, plo = cut(planes[...])
    for n in range(3):
        cols = slice(n * 256, (n + 1) * 256)
        r = dot(ph, sin_r[0, :, cols]) + dot(plo, sin_r[0, :, cols]) + dot(ph, sin_r[1, :, cols])
        planes[:, cols] = r
    for c in range(CH):
        cols = slice(c * LANES, (c + 1) * LANES)
        first, last = solve(lambda z: rhy[z, :, cols], eg, cols, work)
        q0 = planes[0:YL, cols] + first
        q7 = planes[YL : 2 * YL, cols] + last
        there = slice((c % 3) * LANES, (c % 3 + 1) * LANES)
        for rt in range(YL // 8):
            qbuf[2 * rt + c // 3, 0, :, there] = q0[8 * rt : 8 * rt + 8]
            qbuf[2 * rt + c // 3, 1, :, there] = q7[8 * rt : 8 * rt + 8]

    for s, g in enumerate(SOLVERS):

        @pl.when(gz != g)
        def _():
            remote(qbuf.at[s], qrecv.at[gz], qsend_s.at[s], qrecv_s.at[gz], {"gz": g}).start()

        @pl.when(gz == g)
        def _():
            qrecv[gz] = qbuf[s]

    @pl.when(is_solver)
    def _():
        for d in range(1, NB):
            g = peer(gz, d)
            remote(qbuf.at[0], qrecv.at[g], qsend_s.at[0], qrecv_s.at[g], {"gz": g}).wait_recv()
        s = jnp.zeros((8, HALF), F32)
        for b in range(NB):
            rbuf[b, 0] = s
            h = ci[b] * (qrecv[b, 0] + c00[b] * s)
            hh[b] = h
            s = qrecv[b, 1] + c70[b] * s + c70c[b] * h
        value = jnp.zeros((8, HALF), F32)
        for b in range(NB - 1, -1, -1):
            rbuf[b, 1] = value
            if b:
                upper = hh[b] + cia[b] * value
                rbuf[b, 0] = rbuf[b, 0] + cc[b - 1] * upper
                value = upper
        for d in range(1, NB):
            g = peer(gz, d)
            remote(rbuf.at[g], rrecv.at[me_s], rsend_s.at[d], rrecv_s.at[me_s], {"gz": g}).start()
        rrecv[me_s] = rbuf[gz]

    for s, g in enumerate(SOLVERS):

        @pl.when(gz != g)
        def _():
            remote(qbuf.at[s], qrecv.at[gz], qsend_s.at[s], qrecv_s.at[gz], {"gz": g}).wait_send()
            remote(rbuf.at[0], rrecv.at[s], rsend_s.at[0], rrecv_s.at[s], {"gz": g}).wait_recv()

    for c in range(CH):
        cols = slice(c * LANES, (c + 1) * LANES)
        there = slice((c % 3) * LANES, (c % 3 + 1) * LANES)
        low = jnp.concatenate([rrecv[2 * rt + c // 3, 0, :, there] for rt in range(YL // 8)], axis=0)
        high = jnp.concatenate([rrecv[2 * rt + c // 3, 1, :, there] for rt in range(YL // 8)], axis=0)
        planes[0:YL, cols] = low
        planes[YL : 2 * YL, cols] = high

        def full(z):
            r = rhy[z, :, cols]
            if z == 0:
                r = r + a_of(0, tile) * low
            if z == ZL - 1:
                r = r + b_of(ZL - 1, tile) * high
            return r

        solve(full, eg, cols, work)
    a, b = cut(work[...].reshape(ZL * YL, N))
    r = dot(a, wout[0]) + dot(b, wout[0]) + dot(a, wout[1])
    edge = []
    for t in range(2):
        value = near[t]
        for z in range(ZL):
            value = value + jnp.where(at_z[z], r[z * YL : (z + 1) * YL, t * LANES : (t + 1) * LANES], 0.0)
        edge.append(value)
    ph, plo = cut(planes[...])
    for n in range(3):
        cols = slice(n * 256, (n + 1) * 256)
        r = dot(ph, sin_r[0, :, cols]) + dot(plo, sin_r[0, :, cols]) + dot(ph, sin_r[1, :, cols])
        planes[:, cols] = r
    for p in range(NB):
        value = zero
        for half_p in range(2):
            t0 = YL * p // LANES
            for t in range(t0, (YL * p + YL - 1) // LANES + 1):
                shift = LANES * t - YL * p + YL * half_p
                first = max(LANES * t, YL * p) - YL * p + YL * half_p
                stop = min(LANES * (t + 1), YL * p + YL) - YL * p + YL * half_p
                piece = rolled(planes[half_p * YL : (half_p + 1) * YL, t * LANES : (t + 1) * LANES], shift)
                value = jnp.where((lanes >= first) & (lanes < stop), piece, value)
        piece = rolled(edge[p // 8], 2 * YL - 16 * (p % 8))
        value = jnp.where((lanes >= 2 * YL) & (lanes < 2 * YL + 16), piece, value)
        bbuf[p] = value

    bcopies = [
        remote(bbuf.at[peer(pa, d)], mine48(brecv, pa), bsend_s.at[d], brecv_s.at[pa], {"pa": peer(pa, d)})
        for d in range(1, NB)
    ]
    for copy in bcopies:
        copy.start()
    brecv[pl.ds(pl.multiple_of(pa * YL, YL), YL), :] = bbuf[pa]

    rows = lax.broadcasted_iota(jnp.int32, (LANES, LANES), 0)
    scale[...] = jnp.where(
        rows < YL, a_of(0, (LANES, LANES)), jnp.where(rows < 2 * YL, b_of(ZL - 1, (LANES, LANES)), 1.0)
    )
    for copy in bcopies:
        copy.wait_send()

    @pl.when(is_solver)
    def _():
        for d in range(1, NB):
            g = peer(gz, d)
            remote(rbuf.at[g], rrecv.at[me_s], rsend_s.at[d], rrecv_s.at[me_s], {"gz": g}).wait_send()

    for d in range(1, NB):
        p = peer(pa, d)
        remote(bbuf.at[p], mine48(brecv, p), bsend_s.at[d], brecv_s.at[p], {"pa": p}).wait_recv()

    def again(c):
        cols = pl.ds(pl.multiple_of(c * LANES, LANES), LANES)
        x = jnp.transpose(brecv[cols, :]) * scale[...]
        add = table_by(mc[0], mc[1], x)
        solve(lambda z: fh[z, :, cols] + add[z * YL : (z + 1) * YL], eloc, cols, work)
        for z in range(ZL):
            a, b = cut(work[z, :, cols])
            u = dot(s48[...], jnp.concatenate([a, b, a], axis=0))
            a, b = cut(u)
            s_hi[z * YL : (z + 1) * YL, cols] = a
            s_lo[z * YL : (z + 1) * YL, cols] = b

    pl.loop(0, CH)(again)
    for n in range(3):
        cols = slice(n * 256, (n + 1) * 256)
        r = dot(s_hi[...], cos_r[0, :, cols]) + dot(s_lo[...], cos_r[0, :, cols])
        out[:, cols] = r + dot(s_hi[...], cos_r[1, :, cols])


def on_device(source, cell_width):
    t = tables()
    args = [jnp.asarray(t[name]) for name in TABLES]
    vmem = pl.BlockSpec(memory_space=pltpu.VMEM)
    v = pltpu.VMEM
    dma = pltpu.SemaphoreType.DMA
    line = (NB, 8, HALF)
    out = pl.pallas_call(
        kernel,
        out_shape=jax.ShapeDtypeStruct((ZL * YL, N), F32),
        in_specs=[vmem, pl.BlockSpec(memory_space=pltpu.SMEM)] + [vmem] * len(args),
        out_specs=vmem,
        scratch_shapes=[
            v((ZL * YL, N), BF16),
            v((ZL * YL, N), BF16),
            v((ZL, YL, N), F32),
            v((ZL, YL, N), F32),
            v((ZL, YL, N), F32),
            v((N, LANES), F32),
            v((NB, YL, LANES), F32),
            v((ZL, LANES), F32),
            v((NB, ZL, LANES), F32),
            v((NB * ZL, LANES), F32),
            v((NB * ZL, LANES), F32),
            v((2 * YL, N), F32),
            v((ZL, YL, N), F32),
            v((ZL, YL, N), F32),
            v((NS, 2, 8, HALF), F32),
            v((NB, 2, 8, HALF), F32),
            v((NB, 2, 8, HALF), F32),
            v((NS, 2, 8, HALF), F32),
        ]
        + [v(line, F32)] * 7
        + [
            v((NB, YL, LANES), F32),
            v((N, LANES), F32),
            v((LANES, LANES), F32),
        ]
        + [dma((NB,))] * 10,
        compiler_params=pltpu.CompilerParams(
            collective_id=0, has_side_effects=True, vmem_limit_bytes=60 * 1024 * 1024
        ),
        name="poisson",
    )(source.reshape(ZL * YL, N), cell_width, *args)
    return out.reshape(ZL, YL, N)


def solution(mesh):
    return jax.shard_map(
        on_device,
        mesh=mesh,
        in_specs=(P("gz", "pa", None), P("gz")),
        out_specs=P("gz", "pa", None),
        check_vma=False,
    )
```

profile of v0, /device:TPU:1, one launch (start us, length us, event | category | flops | bytes accessed | tf_op | source)
XLA Modules:
  0.0 69.9 jit_solution(894344672509877613)
XLA Ops:
  0.0 67.5 %poisson.1 = f32[384,768]{1,0:T(8,128)} custom-call(f32[384,768]{1,0:T(8,128)} %bitcast.3, f32[8]{0:T(128)} %cw.1, bf16[2,768,768]{2,1,0:T(8,128)(2,1)} %constant.20.clone.cos_r, bf16[2,768,768]{2,1,0:T(8,128)(2,1)} %constant.21.clone.sin_r, bf16[48,144]{1,0:T(8,128)(2,1)} %constant.22.clone.s48, bf16[2,128,384]{2,1,0:T(8,128)(2,1)} %constant.23.clone.mct, ...), custom_call_target="tpu_custom_call" | custom-call | tf_op jit(solution)/shard_map/poisson/pallas_call | solution.py:505
  67.5 2.4 %copy.14 = f32[8,48,768]{2,1,0:T(8,128)} copy(f32[8,48,768]{2,1,0:T(8,128)} %bitcast.2) | data formatting | bytes 2359296
where the time goes:
time: 70 us; the launch traced here: 69.9 us
  Pallas kernels  67.5 us (96%)
  local copies, waits for them, and re-layouts  2.36 us (3%)
    pallas_call x1, Pallas kernels, on_device(): pl.pallas_call(kernel, out_shape=jax.ShapeDtypeStruct((ZL * YL, N), F32),...  67.5 us
    unnamed x1, local copies, waits for them, and re-layouts  2.36 us

commit v1 on v0

v1 whole, which is shorter than its diff:
```python
import functools

import jax
import jax.numpy as jnp
import numpy as np
from jax import lax
from jax.experimental import pallas as pl
from jax.experimental.pallas import tpu as pltpu
from jax.sharding import PartitionSpec as P

F32 = jnp.float32
BF16 = jnp.bfloat16
N = 768
NB = 16
ZL = 8
YL = 48
LANES = 128
CH = N // LANES
NC = 3
CW = N // NC
KB = CW // NB
IDLE = (0, 4, 10, 14)
SOLVERS = tuple(g for g in range(NB) if g not in IDLE)
NS = len(SOLVERS)


def split64(x):
    hi = x.astype(np.float32).astype(jnp.bfloat16)
    lo = (x - hi.astype(np.float64)).astype(np.float32).astype(jnp.bfloat16)
    return np.stack([hi, lo])


@functools.cache
def tables():
    n = np.arange(N)
    phases = n[:, None] * (2 * n[None, :] + 1) % (4 * N)
    weights = np.where(n == 0, np.sqrt(1.0 / N), np.sqrt(2.0 / N))
    cos_t = weights[:, None] * np.cos(phases * (np.pi / (2 * N)))

    def sine(width, rows, cols):
        p = rows[:, None] * cols[None, :] % (2 * (width + 1))
        return np.sqrt(2.0 / (width + 1)) * np.sin(p * (np.pi / (width + 1)))

    m = n + 1
    sin_t = sine(N, m, m)
    ml = np.arange(1, YL + 1)
    s48 = sine(YL, ml, ml)
    hi, lo = split64(s48)
    s48st = np.concatenate([hi, hi, lo], axis=1)
    mc = np.zeros((ZL * YL, LANES))
    mc[:YL, :YL] = s48
    mc[(ZL - 1) * YL :, YL : 2 * YL] = s48
    for z in range(ZL):
        mc[z * YL : (z + 1) * YL, 2 * YL + 2 * z] = s48[:, 0]
        mc[z * YL : (z + 1) * YL, 2 * YL + 2 * z + 1] = s48[:, YL - 1]
    own = np.zeros((NB, ZL, 2, N))
    beside = np.zeros((NB, ZL, 2, N))
    for p in range(NB):
        for e in range(2):
            row = YL * p + (YL - 1) * e
            own[p, :, e] = sin_t[row]
            near = row + (1 if e else -1)
            if 0 <= near < N:
                beside[p, :, e] = sin_t[near]
    own = own.reshape(2 * ZL * NB, N)
    beside = beside.reshape(2 * ZL * NB, N)
    lam_k = 4 * np.sin(n * np.pi / (2 * N)) ** 2
    lam_l = 4 * np.sin(m * np.pi / (2 * (N + 1))) ** 2
    lam_s = 4 * np.sin(ml * np.pi / (2 * (YL + 1))) ** 2
    rows = np.zeros((8, N), np.float32)
    rows[0] = lam_k
    rows[1] = lam_l
    cos2 = split64(cos_t)
    return dict(
        fwd=np.ascontiguousarray(cos2.reshape(2, NC, CW, N).transpose(1, 0, 3, 2)),
        bwd=np.ascontiguousarray(cos2.reshape(2, NC, CW, N).transpose(1, 0, 2, 3)),
        sin=split64(sin_t),
        s48=s48st,
        mct=split64(mc.T.copy()),
        mc=split64(mc),
        win=split64(own),
        wout=split64(beside.T.copy()),
        rows=rows,
        lam_s=np.broadcast_to(lam_s[:, None], (YL, CW)).astype(np.float32),
        lam_k=np.broadcast_to(lam_k[:, None], (N, LANES)).astype(np.float32).reshape(NC * NB, KB, LANES),
    )


TABLES = ("fwd", "bwd", "sin", "s48", "mct", "mc", "win", "wout", "rows", "lam_s", "lam_k")


def cut(x):
    hi = x.astype(BF16)
    return hi, (x - hi.astype(F32)).astype(BF16)


def dot(a, b):
    return jnp.dot(a, b, preferred_element_type=F32)


def by_table(a, b, hi, lo):
    return dot(a, hi) + dot(b, hi) + dot(a, lo)


def table_by(hi, lo, x):
    a, b = cut(x)
    return dot(hi, a) + dot(hi, b) + dot(lo, a)


def recip(x):
    return 1.0 / x


def remote(src, dst, send, recv, where):
    return pltpu.make_async_remote_copy(
        src_ref=src,
        dst_ref=dst,
        send_sem=send,
        recv_sem=recv,
        device_id=where,
        device_id_type=pl.DeviceIdType.MESH,
    )


def rolled(x, shift):
    shift %= LANES
    return x if shift == 0 else pltpu.roll(x, shift, axis=1)


def wide(row, like):
    return jnp.broadcast_to(jnp.concatenate([row] * (like[1] // LANES), axis=1), like)


def kernel(
    src_h, cw, fwd_h, bwd_h, sin_h, s48_h, mct_h, mc_h, win_h, wout_h, rows_h, lam_s_h, lam_k_h, out,
    src, fwd, bwd, sin_r, s48, mct, mc, win, wout, lam_rows, lam_s, lam_k,
    s_hi, s_lo, fh, work, eloc, pbuf, precv, wmine, widths, alpha, beta, r_before, r_after,
    rhy, eg, gwork, qbuf, qrecv, rbuf, rrecv, ks, ku0, ku7, kv0, kv7, kh, kia, kc, hh, ss, bbuf, brecv,
    load_s, psend_s, precv_s, wsend_s, wrecv_s, qsend_s, qrecv_s, rsend_s, rrecv_s, bsend_s, brecv_s,
):
    pa = lax.axis_index("pa")
    gz = lax.axis_index("gz")

    def peer(me, d):
        return lax.rem(me + d, NB)

    loads = {}

    def load(name, h, v):
        loads[name] = pltpu.make_async_copy(h, v, load_s.at[len(loads)])
        loads[name].start()

    def need(*names):
        for name in names:
            loads[name].wait()

    load("src", src_h, src)
    load("fwd0", fwd_h.at[0], fwd.at[0])
    load("s48", s48_h, s48)
    load("rows", rows_h, lam_rows)
    load("lam_s", lam_s_h, lam_s)
    load("mct", mct_h, mct)
    for c in range(NC):
        load("lam_k%d" % c, lam_k_h.at[NB * c + pa], lam_k.at[c])

    barrier = pltpu.get_barrier_semaphore()
    for d in range(1, NB):
        pl.semaphore_signal(barrier, inc=1, device_id={"pa": peer(pa, d)}, device_id_type=pl.DeviceIdType.MESH)
        pl.semaphore_signal(barrier, inc=1, device_id={"gz": peer(gz, d)}, device_id_type=pl.DeviceIdType.MESH)

    for z in range(ZL):
        wmine[z : z + 1, :] = jnp.full((1, LANES), cw[z], F32)
    w = wmine[...]
    at = lax.broadcasted_iota(jnp.int32, (ZL, LANES), 0)
    al_b = 2.0 / ((jnp.where(at == 0, w, pltpu.roll(w, 1, axis=0)) + w) * w)
    be_b = 2.0 / ((w + jnp.where(at == ZL - 1, w, pltpu.roll(w, ZL - 1, axis=0))) * w)

    def a_of(z, like):
        return wide(al_b[z : z + 1, :], like)

    def b_of(z, like):
        return wide(be_b[z : z + 1, :], like)

    def factor(e_ref, lam):
        like = lam.shape
        e = None
        for z in range(ZL):
            d = a_of(z, like) + b_of(z, like) + lam
            if z:
                d = d - a_of(z, like) * b_of(z - 1, like) * e
            e = recip(d)
            e_ref[z] = e

    def solve(rhs_of, e_ref, x_ref):
        like = x_ref.shape[1:]
        y = None
        for z in range(ZL):
            r = rhs_of(z)
            if z:
                r = r + a_of(z, like) * y
            y = e_ref[z] * r
            x_ref[z] = y
        last = y
        for z in range(ZL - 2, -1, -1):
            y = x_ref[z] + e_ref[z] * b_of(z, like) * y
            x_ref[z] = y
        return y, last

    need("src", "fwd0", "s48")
    load("fwd1", fwd_h.at[1], fwd.at[1])
    load("fwd2", fwd_h.at[2], fwd.at[2])
    s_hi[...], s_lo[...] = cut(src[...])

    def sines(x):
        a, b = cut(x)
        return dot(s48[...], jnp.concatenate([a, b, a], axis=0))

    def block(c):
        f = by_table(s_hi[...], s_lo[...], fwd[c, 0], fwd[c, 1])
        for z in range(ZL):
            fh[c, z] = sines(f[z * YL : (z + 1) * YL])
        if c == 0:
            need("rows", "lam_s", "mct")
        factor(eloc.at[c], lam_s[...] + lam_rows[0:1, c * CW : (c + 1) * CW])
        solve(lambda z: fh[c, z], eloc.at[c], work.at[c])
        p = table_by(mct[0], mct[1], work[c].reshape(ZL * YL, CW))
        for t in range(CW // LANES):
            cols = slice(t * LANES, (t + 1) * LANES)
            pbuf[c, cols, :] = jnp.transpose(p[:, cols])

    def mine(ref, c, q):
        return ref.at[c, pl.ds(pl.multiple_of(q * KB, KB), KB), :]

    copies = []

    def start(copy):
        copies.append(copy)
        copy.start()

    def send_perimeter(c):
        for d in range(1, NB):
            q = peer(pa, d)
            start(remote(mine(pbuf, c, q), precv.at[c, pa], psend_s.at[c, d], precv_s.at[c, pa], {"pa": q}))
        precv[c, pa] = pbuf[c, pl.ds(pl.multiple_of(pa * KB, KB), KB), :]

    for c in range(NC):
        if c:
            need("fwd%d" % c)
        block(c)
        if c == 0:
            load("win", win_h, win)
            load("sin", sin_h, sin_r)
            load("wout", wout_h, wout)
            load("mc", mc_h, mc)
            load("bwd", bwd_h, bwd)
            pl.semaphore_wait(barrier, 2 * (NB - 1))
        send_perimeter(c)
        if c == 0:
            for d in range(1, NB):
                start(remote(wmine, widths.at[gz], wsend_s.at[d], wrecv_s.at[gz], {"gz": peer(gz, d)}))
            widths[gz] = wmine[...]

    need(*("lam_k%d" % c for c in range(NC)))
    for c in range(NC):
        factor(eg.at[c], wide(lam_k[c], (KB, N)) + lam_rows[1:2, :])

    for d in range(1, NB):
        g = peer(gz, d)
        remote(wmine, widths.at[g], wsend_s.at[d], wrecv_s.at[g], {"gz": g}).wait_recv()
    w = widths[...].reshape(NB * ZL, LANES)
    at = lax.broadcasted_iota(jnp.int32, (NB * ZL, LANES), 0)
    before = jnp.where(at == 0, 0.0, pltpu.roll(w, 1, axis=0))
    after = jnp.where(at == NB * ZL - 1, 0.0, pltpu.roll(w, NB * ZL - 1, axis=0))
    alpha[...] = 2.0 / ((before + w) * w)
    beta[...] = 2.0 / ((w + after) * w)
    r_before[...] = (before - w) / (2.0 * w)
    r_after[...] = (after - w) / (2.0 * w)

    me_s = gz - sum(((gz > g).astype(jnp.int32) for g in IDLE), jnp.int32(0))
    is_solver = functools.reduce(lambda x, y: x & y, [gz != g for g in IDLE])
    line = (8 * NC, LANES)

    def row_of(ref, i):
        return jnp.broadcast_to(ref[pl.ds(i, 1), :], line)

    @pl.when(is_solver)
    def _():
        rt = lax.div(me_s, CH)
        lt = lax.rem(me_s, CH)
        lam = jnp.concatenate([lam_k[c, pl.ds(pl.multiple_of(8 * rt, 8), 8), :] for c in range(NC)], axis=0)
        lam = lam + lam_rows[1:2, pl.ds(pl.multiple_of(lt * LANES, LANES), LANES)]

        def coefficients(b, carry):
            al = [row_of(alpha, b * ZL + z) for z in range(ZL)]
            be = [row_of(beta, b * ZL + z) for z in range(ZL)]
            e = recip(al[0] + be[0] + lam)
            prod_e = e
            prod_b = be[0]
            for z in range(1, ZL):
                e = recip(al[z] + be[z] + lam - al[z] * be[z - 1] * e)
                prod_e = prod_e * e * al[z]
                prod_b = prod_b * be[z] / al[z]
            g = recip(al[ZL - 1] + be[ZL - 1] + lam)
            for z in range(ZL - 2, -1, -1):
                g = recip(al[z] + be[z] + lam - be[z] * al[z + 1] * g)
            kh[b] = g * al[0]
            ks[b] = prod_e * al[0]
            kia[b] = prod_e * prod_b
            kc[b] = e * be[ZL - 1]
            return carry

        lax.fori_loop(0, NB, coefficients, 0)
        c = jnp.zeros(line, F32)
        for b in range(NB):
            a00, a70, a07, a77 = kh[b], ks[b], kia[b], kc[b]
            inv = recip(1.0 - a00 * c)
            mixed = a70 * c * inv
            rb = row_of(r_before, b * ZL)
            ra = row_of(r_after, b * ZL + ZL - 1)
            p00 = 1.0 + a00 * rb
            p07 = a07 * ra
            ku0[b] = a70 * rb + mixed * p00
            ku7[b] = 1.0 + a77 * ra + mixed * p07
            kv0[b] = inv * p00
            kv7[b] = inv * p07
            ks[b] = a70 * inv
            kh[b] = a00 * inv
            kia[b] = a07 * inv
            c = a77 + mixed * a07
            kc[b] = c

    small = (KB, LANES)
    lanes = lax.broadcasted_iota(jnp.int32, small, 1)
    odd = lax.rem(lanes, 2) == 1
    at_z = [lax.div(lax.rem(lanes, 16), 2) == z for z in range(ZL)]
    zero = jnp.zeros(small, F32)
    near = {}

    def ends(c):
        for d in range(1, NB):
            p = peer(pa, d)
            remote(mine(pbuf, c, p), precv.at[c, p], psend_s.at[c, d], precv_s.at[c, p], {"pa": p}).wait_recv()

        def gathered(base, t):
            value = zero
            for p in range(NB):
                first = YL * p - LANES * t
                if first + YL <= 0 or first >= LANES:
                    continue
                piece = rolled(precv[c, p], first - base)
                value = jnp.where((lanes >= first) & (lanes < first + YL), piece, value)
            return value

        def beside(t):
            value = zero
            for p in range(8 * t, 8 * t + 8):
                at_p = lax.div(lanes, 16) == p - 8 * t
                first = 16 * (p - 8 * t) - 2 * YL
                if p > 0:
                    value = jnp.where(at_p & ~odd, rolled(precv[c, p - 1], first - 1), value)
                if p < NB - 1:
                    value = jnp.where(at_p & odd, rolled(precv[c, p + 1], first + 1), value)
            return value

        planes = jnp.concatenate(
            [jnp.concatenate([gathered(base, t) for t in range(CH)], axis=1) for base in (0, YL)], axis=0
        )
        near[c] = [beside(t) for t in range(2)]
        rows = jnp.concatenate(
            [jnp.concatenate([jnp.where(at_z[z], v, 0.0) for v in near[c]], axis=1) for z in range(ZL)], axis=0
        )
        if c == 0:
            need("win", "sin")
        rhy[c] = by_table(*cut(rows), win[0], win[1]).reshape(ZL, KB, N)
        v = by_table(*cut(planes), sin_r[0], sin_r[1])
        first, last = solve(lambda z: rhy[c, z], eg.at[c], gwork.at[c])
        q = (v[0:KB] + first, v[KB : 2 * KB] + last)
        for s in range(NS):
            rt, lt = divmod(s, CH)
            for i in range(2):
                qbuf[c, s, i] = q[i][8 * rt : 8 * rt + 8, lt * LANES : (lt + 1) * LANES]
        for s, g in enumerate(SOLVERS):

            @pl.when(gz != g)
            def _():
                remote(qbuf.at[c, s], qrecv.at[c, gz], qsend_s.at[c, s], qrecv_s.at[c, gz], {"gz": g}).start()

            @pl.when(gz == g)
            def _():
                qrecv[c, gz] = qbuf[c, s]

    def chain(c):
        for d in range(1, NB):
            g = peer(gz, d)
            remote(qbuf.at[c, 0], qrecv.at[c, g], qsend_s.at[c, 0], qrecv_s.at[c, g], {"gz": g}).wait_recv()
        part = slice(8 * c, 8 * c + 8)

        def row8(ref, i):
            return jnp.broadcast_to(ref[i : i + 1, :], (8, LANES))

        s = None
        for b in range(NB):
            q0, q7 = qrecv[c, b, 0], qrecv[c, b, 1]
            h = kv0[b, part] * q0 + kv7[b, part] * q7
            v = ku0[b, part] * q0 + ku7[b, part] * q7
            if b:
                h = h + kh[b, part] * s
                v = v + ks[b, part] * s
            s = v
            hh[b] = h
            ss[b] = s
        upper = None
        for b in range(NB - 1, -1, -1):
            head = hh[b]
            tail = ss[b]
            if b < NB - 1:
                head = head + kia[b, part] * upper
                tail = tail + kc[b, part] * upper
            hh[b] = head
            ss[b] = tail
            upper = head
        for b in range(NB):
            low = row8(r_before, b * ZL) * hh[b]
            if b:
                low = low + ss[b - 1]
            high = row8(r_after, b * ZL + ZL - 1) * ss[b]
            if b < NB - 1:
                high = high + hh[b + 1]
            rbuf[c, b, 0] = row8(alpha, b * ZL) * low
            rbuf[c, b, 1] = row8(beta, b * ZL + ZL - 1) * high
        for d in range(1, NB):
            g = peer(gz, d)
            remote(rbuf.at[c, g], rrecv.at[c, me_s], rsend_s.at[c, d], rrecv_s.at[c, me_s], {"gz": g}).start()
        rrecv[c, me_s] = rbuf[c, gz]

    def inner(c):
        for s, g in enumerate(SOLVERS):

            @pl.when(gz != g)
            def _():
                remote(qbuf.at[c, s], rrecv.at[c, s], qsend_s.at[c, s], rrecv_s.at[c, s], {"gz": g}).wait_recv()

        low, high = (
            jnp.concatenate(
                [jnp.concatenate([rrecv[c, CH * rt + lt, i] for lt in range(CH)], axis=1) for rt in range(2)], axis=0
            )
            for i in range(2)
        )
        ends_of = {0: low, ZL - 1: high}
        solve(lambda z: rhy[c, z] + ends_of[z] if z in ends_of else rhy[c, z], eg.at[c], gwork.at[c])
        if c == 0:
            need("wout")
        r = by_table(*cut(gwork[c].reshape(ZL * KB, N)), wout[0], wout[1])
        planes = by_table(*cut(jnp.concatenate([low, high], axis=0)), sin_r[0], sin_r[1])
        edge = []
        for t in range(2):
            value = near[c][t]
            for z in range(ZL):
                value = value + jnp.where(at_z[z], r[z * KB : (z + 1) * KB, t * LANES : (t + 1) * LANES], 0.0)
            edge.append(value)
        for p in range(NB):
            value = zero
            for e in range(2):
                for t in range(YL * p // LANES, (YL * p + YL - 1) // LANES + 1):
                    move = YL * e - YL * p
                    first = max(LANES * t, YL * p) + move
                    stop = min(LANES * (t + 1), YL * p + YL) + move
                    piece = rolled(planes[e * KB : (e + 1) * KB, t * LANES : (t + 1) * LANES], LANES * t + move)
                    value = jnp.where((lanes >= first) & (lanes < stop), piece, value)
            piece = rolled(edge[p // 8], 2 * YL - 16 * (p % 8))
            bbuf[c, p] = jnp.where((lanes >= 2 * YL) & (lanes < 2 * YL + 16), piece, value)
        for d in range(1, NB):
            p = peer(pa, d)
            start(remote(bbuf.at[c, p], mine(brecv, c, pa), bsend_s.at[c, d], brecv_s.at[c, pa], {"pa": p}))
        brecv[c, pl.ds(pl.multiple_of(pa * KB, KB), KB), :] = bbuf[c, pa]

    def again(c):
        for d in range(1, NB):
            p = peer(pa, d)
            remote(bbuf.at[c, p], mine(brecv, c, p), bsend_s.at[c, d], brecv_s.at[c, p], {"pa": p}).wait_recv()
        if c == 0:
            need("mc", "bwd")
        x = jnp.concatenate(
            [jnp.transpose(brecv[c, t * LANES : (t + 1) * LANES, :]) for t in range(CW // LANES)], axis=1
        )
        add = table_by(mc[0], mc[1], x)
        solve(lambda z: fh[c, z] + add[z * YL : (z + 1) * YL], eloc.at[c], work.at[c])
        u = jnp.concatenate([sines(work[c, z]) for z in range(ZL)], axis=0)
        part = by_table(*cut(u), bwd[c, 0], bwd[c, 1])
        if c == 0:
            out[...] = part
        else:
            out[...] += part

    for c in range(NC):
        ends(c)
    for c in range(NC):
        pl.when(is_solver)(functools.partial(chain, c))
    for c in range(NC):
        inner(c)
    for c in range(NC):
        again(c)

    for copy in copies:
        copy.wait_send()
    for c in range(NC):
        for s, g in enumerate(SOLVERS):

            @pl.when(gz != g)
            def _():
                remote(qbuf.at[c, s], qrecv.at[c, gz], qsend_s.at[c, s], qrecv_s.at[c, gz], {"gz": g}).wait_send()

        @pl.when(is_solver)
        def _():
            for d in range(1, NB):
                g = peer(gz, d)
                remote(rbuf.at[c, g], rrecv.at[c, me_s], rsend_s.at[c, d], rrecv_s.at[c, me_s], {"gz": g}).wait_send()


def on_device(source, cell_width):
    t = tables()
    args = [jnp.asarray(t[name]) for name in TABLES]
    hbm = pl.BlockSpec(memory_space=pltpu.HBM)
    v = pltpu.VMEM
    dma = pltpu.SemaphoreType.DMA
    here = [v(x.shape, x.dtype) for x in args[:-1]] + [v((NC, KB, LANES), F32)]
    coef = v((NB, 8 * NC, LANES), F32)
    out = pl.pallas_call(
        kernel,
        out_shape=jax.ShapeDtypeStruct((ZL * YL, N), F32),
        in_specs=[hbm, pl.BlockSpec(memory_space=pltpu.SMEM)] + [hbm] * len(args),
        out_specs=pl.BlockSpec(memory_space=pltpu.VMEM),
        scratch_shapes=[v((ZL * YL, N), F32)]
        + here
        + [
            v((ZL * YL, N), BF16),
            v((ZL * YL, N), BF16),
            v((NC, ZL, YL, CW), F32),
            v((NC, ZL, YL, CW), F32),
            v((NC, ZL, YL, CW), F32),
            v((NC, CW, LANES), F32),
            v((NC, NB, KB, LANES), F32),
            v((ZL, LANES), F32),
            v((NB, ZL, LANES), F32),
        ]
        + [v((NB * ZL, LANES), F32)] * 4
        + [
            v((NC, ZL, KB, N), F32),
            v((NC, ZL, KB, N), F32),
            v((NC, ZL, KB, N), F32),
            v((NC, NS, 2, 8, LANES), F32),
            v((NC, NB, 2, 8, LANES), F32),
            v((NC, NB, 2, 8, LANES), F32),
            v((NC, NS, 2, 8, LANES), F32),
        ]
        + [coef] * 8
        + [
            v((NB, 8, LANES), F32),
            v((NB, 8, LANES), F32),
            v((NC, NB, KB, LANES), F32),
            v((NC, CW, LANES), F32),
            dma((24,)),
            dma((NC, NB)),
            dma((NC, NB)),
            dma((NB,)),
            dma((NB,)),
        ]
        + [dma((NC, NB))] * 6,
        compiler_params=pltpu.CompilerParams(
            collective_id=0, has_side_effects=True, vmem_limit_bytes=44 * 1024 * 1024
        ),
        name="poisson",
    )(*(pltpu.with_memory_space_constraint(x, pltpu.HBM) for x in (source.reshape(ZL * YL, N), cell_width, *args)))
    return out.reshape(ZL, YL, N)


def solution(mesh):
    return jax.shard_map(
        on_device,
        mesh=mesh,
        in_specs=(P("gz", "pa", None), P("gz")),
        out_specs=P("gz", "pa", None),
        check_vma=False,
    )
```

time: 70 us -> 50.8 us (0.73)
  Pallas kernels: 67.5 us -> 49.7 us
  local copies, waits for them, and re-layouts: 2.36 us -> 1.02 us
    pallas_call x1, Pallas kernels: 67.5 us -> 49.7 us  [on_device(): pl.pallas_call(kernel, out_shape=jax.ShapeDtypeStruct((ZL * YL, N), F32),...]
    unnamed x1, local copies, waits for them, and re-layouts: 2.36 us -> 1.02 us
where the time goes in v1:
time: 50.8 us; the launch traced here: 50.7 us
  Pallas kernels  49.7 us (98%)
  local copies, waits for them, and re-layouts  1.02 us (2%)
    pallas_call x1, Pallas kernels, on_device(): pl.pallas_call(kernel, out_shape=jax.ShapeDtypeStruct((ZL * YL, N), F32),...  49.7 us

profile of v1, /device:TPU:1, one launch (start us, length us, event | category | flops | bytes accessed | tf_op | source)
XLA Modules:
  0.0 50.7 jit_solution(10447266864154239607)
XLA Ops:
  0.0 49.7 %poisson.1 = f32[384,768]{1,0:T(8,128)S(1)} custom-call(f32[384,768]{1,0:T(8,128)} %bitcast.3, f32[8]{0:T(128)} %cw.1, bf16[3,2,768,256]{3,2,1,0:T(8,128)(2,1)} %constant.22.clone.fwd_h, bf16[3,2,256,768]{3,2,1,0:T(8,128)(2,1)} %constant.23.clone.bwd_h, bf16[2,768,768]{2,1,0:T(8,128)(2,1)} %constant.24.clone.sin_h, bf16[48,144]{1,0:T(8,128)(2,1)} %constant.25.clone.s48_h, ...), custom_call_target="tpu_custom_call" | custom-call | tf_op jit(solution)/shard_map/poisson/pallas_call | solution.py:528
  49.7 1.0 %copy.15 = f32[8,48,768]{2,1,0:T(8,128)} copy(f32[8,48,768]{2,1,0:T(8,128)S(1)} %bitcast.2) | data formatting | bytes 2359296

commit v2 on v1

--- a/solution.py
+++ b/solution.py
@@ -20,6 +20,8 @@
 CW = N // NC
 KB = CW // NB
 IDLE = (0, 4, 10, 14)
+PA_ORDER = (4, 12, 3, 5, 11, 13, 2, 6, 10, 14, 1, 7, 9, 15, 8)
+GZ_ORDER = (12, 4, 11, 13, 5, 3, 10, 14, 6, 2, 7, 9, 8, 15, 1)
 SOLVERS = tuple(g for g in range(NB) if g not in IDLE)
 NS = len(SOLVERS)
 
@@ -76,8 +78,8 @@
         bwd=np.ascontiguousarray(cos2.reshape(2, NC, CW, N).transpose(1, 0, 2, 3)),
         sin=split64(sin_t),
         s48=s48st,
-        mct=split64(mc.T.copy()),
-        mc=split64(mc),
+        mct=split64(mc.T.copy()).reshape(2 * LANES, ZL * YL),
+        mc=split64(mc).reshape(2 * ZL * YL, LANES),
         win=split64(own),
         wout=split64(beside.T.copy()),
         rows=rows,
@@ -98,13 +100,18 @@
     return jnp.dot(a, b, preferred_element_type=F32)
 
 
-def by_table(a, b, hi, lo):
-    return dot(a, hi) + dot(b, hi) + dot(a, lo)
-
-
-def table_by(hi, lo, x):
+def by_table(x, hi, lo):
     a, b = cut(x)
-    return dot(hi, a) + dot(hi, b) + dot(lo, a)
+    m = x.shape[0]
+    r = dot(jnp.concatenate([a, b], axis=0), hi)
+    return r[:m] + r[m:] + dot(a, lo)
+
+
+def table_by(t, x):
+    a, b = cut(x)
+    m = t.shape[0] // 2
+    r = dot(t, a)
+    return r[:m] + r[m:] + dot(t[:m], b)
 
 
 def recip(x):
@@ -136,7 +143,7 @@
     src, fwd, bwd, sin_r, s48, mct, mc, win, wout, lam_rows, lam_s, lam_k,
     s_hi, s_lo, fh, work, eloc, pbuf, precv, wmine, widths, alpha, beta, r_before, r_after,
     rhy, eg, gwork, qbuf, qrecv, rbuf, rrecv, ks, ku0, ku7, kv0, kv7, kh, kia, kc, hh, ss, bbuf, brecv,
-    load_s, psend_s, precv_s, wsend_s, wrecv_s, qsend_s, qrecv_s, rsend_s, rrecv_s, bsend_s, brecv_s,
+    load_s, send_s, recv_s, psend_s, precv_s, qsend_s, qrecv_s, rsend_s, rrecv_s, bsend_s, brecv_s,
 ):
     pa = lax.axis_index("pa")
     gz = lax.axis_index("gz")
@@ -154,11 +161,11 @@
         for name in names:
             loads[name].wait()
 
+    load("rows", rows_h, lam_rows)
+    load("lam_s", lam_s_h, lam_s)
     load("src", src_h, src)
     load("fwd0", fwd_h.at[0], fwd.at[0])
     load("s48", s48_h, s48)
-    load("rows", rows_h, lam_rows)
-    load("lam_s", lam_s_h, lam_s)
     load("mct", mct_h, mct)
     for c in range(NC):
         load("lam_k%d" % c, lam_k_h.at[NB * c + pa], lam_k.at[c])
@@ -206,6 +213,9 @@
             x_ref[z] = y
         return y, last
 
+    need("rows", "lam_s")
+    for c in range(NC):
+        factor(eloc.at[c], lam_s[...] + lam_rows[0:1, c * CW : (c + 1) * CW])
     need("src", "fwd0", "s48")
     load("fwd1", fwd_h.at[1], fwd.at[1])
     load("fwd2", fwd_h.at[2], fwd.at[2])
@@ -216,14 +226,13 @@
         return dot(s48[...], jnp.concatenate([a, b, a], axis=0))
 
     def block(c):
-        f = by_table(s_hi[...], s_lo[...], fwd[c, 0], fwd[c, 1])
+        f = dot(s_hi[...], fwd[c, 0]) + dot(s_lo[...], fwd[c, 0]) + dot(s_hi[...], fwd[c, 1])
         for z in range(ZL):
             fh[c, z] = sines(f[z * YL : (z + 1) * YL])
         if c == 0:
-            need("rows", "lam_s", "mct")
-        factor(eloc.at[c], lam_s[...] + lam_rows[0:1, c * CW : (c + 1) * CW])
+            need("mct")
         solve(lambda z: fh[c, z], eloc.at[c], work.at[c])
-        p = table_by(mct[0], mct[1], work[c].reshape(ZL * YL, CW))
+        p = table_by(mct[...], work[c].reshape(ZL * YL, CW))
         for t in range(CW // LANES):
             cols = slice(t * LANES, (t + 1) * LANES)
             pbuf[c, cols, :] = jnp.transpose(p[:, cols])
@@ -231,16 +240,13 @@
     def mine(ref, c, q):
         return ref.at[c, pl.ds(pl.multiple_of(q * KB, KB), KB), :]
 
-    copies = []
-
-    def start(copy):
-        copies.append(copy)
-        copy.start()
+    def wait_all(ref, sem):
+        pltpu.make_async_copy(ref, ref, sem).wait()
 
     def send_perimeter(c):
-        for d in range(1, NB):
+        for d in PA_ORDER:
             q = peer(pa, d)
-            start(remote(mine(pbuf, c, q), precv.at[c, pa], psend_s.at[c, d], precv_s.at[c, pa], {"pa": q}))
+            remote(mine(pbuf, c, q), precv.at[c, pa], psend_s.at[c], precv_s.at[c], {"pa": q}).start()
         precv[c, pa] = pbuf[c, pl.ds(pl.multiple_of(pa * KB, KB), KB), :]
 
     for c in range(NC):
@@ -256,17 +262,15 @@
             pl.semaphore_wait(barrier, 2 * (NB - 1))
         send_perimeter(c)
         if c == 0:
-            for d in range(1, NB):
-                start(remote(wmine, widths.at[gz], wsend_s.at[d], wrecv_s.at[gz], {"gz": peer(gz, d)}))
+            for d in GZ_ORDER:
+                remote(wmine, widths.at[gz], send_s.at[0], recv_s.at[0], {"gz": peer(gz, d)}).start()
             widths[gz] = wmine[...]
 
     need(*("lam_k%d" % c for c in range(NC)))
     for c in range(NC):
         factor(eg.at[c], wide(lam_k[c], (KB, N)) + lam_rows[1:2, :])
 
-    for d in range(1, NB):
-        g = peer(gz, d)
-        remote(wmine, widths.at[g], wsend_s.at[d], wrecv_s.at[g], {"gz": g}).wait_recv()
+    wait_all(widths.at[0 : NB - 1], recv_s.at[0])
     w = widths[...].reshape(NB * ZL, LANES)
     at = lax.broadcasted_iota(jnp.int32, (NB * ZL, LANES), 0)
     before = jnp.where(at == 0, 0.0, pltpu.roll(w, 1, axis=0))
@@ -276,8 +280,14 @@
     r_before[...] = (before - w) / (2.0 * w)
     r_after[...] = (after - w) / (2.0 * w)
 
-    me_s = gz - sum(((gz > g).astype(jnp.int32) for g in IDLE), jnp.int32(0))
-    is_solver = functools.reduce(lambda x, y: x & y, [gz != g for g in IDLE])
+    def place(g):
+        return g - sum(((g > i).astype(jnp.int32) for i in IDLE), jnp.int32(0))
+
+    def solves(g):
+        return functools.reduce(lambda x, y: x & y, [g != i for i in IDLE])
+
+    me_s = place(gz)
+    is_solver = solves(gz)
     line = (8 * NC, LANES)
 
     def row_of(ref, i):
@@ -337,9 +347,7 @@
     near = {}
 
     def ends(c):
-        for d in range(1, NB):
-            p = peer(pa, d)
-            remote(mine(pbuf, c, p), precv.at[c, p], psend_s.at[c, d], precv_s.at[c, p], {"pa": p}).wait_recv()
+        wait_all(precv.at[c, 0 : NB - 1], precv_s.at[c])
 
         def gathered(base, t):
             value = zero
@@ -371,28 +379,27 @@
         )
         if c == 0:
             need("win", "sin")
-        rhy[c] = by_table(*cut(rows), win[0], win[1]).reshape(ZL, KB, N)
-        v = by_table(*cut(planes), sin_r[0], sin_r[1])
+        rhy[c] = by_table(rows, win[0], win[1]).reshape(ZL, KB, N)
+        v = by_table(planes, sin_r[0], sin_r[1])
         first, last = solve(lambda z: rhy[c, z], eg.at[c], gwork.at[c])
         q = (v[0:KB] + first, v[KB : 2 * KB] + last)
         for s in range(NS):
             rt, lt = divmod(s, CH)
             for i in range(2):
                 qbuf[c, s, i] = q[i][8 * rt : 8 * rt + 8, lt * LANES : (lt + 1) * LANES]
-        for s, g in enumerate(SOLVERS):
-
-            @pl.when(gz != g)
+        for d in GZ_ORDER:
+            g = peer(gz, d)
+
+            @pl.when(solves(g))
             def _():
-                remote(qbuf.at[c, s], qrecv.at[c, gz], qsend_s.at[c, s], qrecv_s.at[c, gz], {"gz": g}).start()
-
-            @pl.when(gz == g)
-            def _():
-                qrecv[c, gz] = qbuf[c, s]
+                remote(qbuf.at[c, place(g)], qrecv.at[c, gz], qsend_s.at[c], qrecv_s.at[c], {"gz": g}).start()
+
+        @pl.when(is_solver)
+        def _():
+            qrecv[c, gz] = qbuf[c, me_s]
 
     def chain(c):
-        for d in range(1, NB):
-            g = peer(gz, d)
-            remote(qbuf.at[c, 0], qrecv.at[c, g], qsend_s.at[c, 0], qrecv_s.at[c, g], {"gz": g}).wait_recv()
+        wait_all(qrecv.at[c, 0 : NB - 1], qrecv_s.at[c])
         part = slice(8 * c, 8 * c + 8)
 
         def row8(ref, i):
@@ -428,17 +435,19 @@
                 high = high + hh[b + 1]
             rbuf[c, b, 0] = row8(alpha, b * ZL) * low
             rbuf[c, b, 1] = row8(beta, b * ZL + ZL - 1) * high
-        for d in range(1, NB):
+        for d in GZ_ORDER:
             g = peer(gz, d)
-            remote(rbuf.at[c, g], rrecv.at[c, me_s], rsend_s.at[c, d], rrecv_s.at[c, me_s], {"gz": g}).start()
+            remote(rbuf.at[c, g], rrecv.at[c, me_s], rsend_s.at[c], rrecv_s.at[c], {"gz": g}).start()
         rrecv[c, me_s] = rbuf[c, gz]
 
     def inner(c):
-        for s, g in enumerate(SOLVERS):
-
-            @pl.when(gz != g)
-            def _():
-                remote(qbuf.at[c, s], rrecv.at[c, s], qsend_s.at[c, s], rrecv_s.at[c, s], {"gz": g}).wait_recv()
+        @pl.when(is_solver)
+        def _():
+            wait_all(rrecv.at[c, 0 : NS - 1], rrecv_s.at[c])
+
+        @pl.when(jnp.logical_not(is_solver))
+        def _():
+            wait_all(rrecv.at[c], rrecv_s.at[c])
 
         low, high = (
             jnp.concatenate(
@@ -450,8 +459,8 @@
         solve(lambda z: rhy[c, z] + ends_of[z] if z in ends_of else rhy[c, z], eg.at[c], gwork.at[c])
         if c == 0:
             need("wout")
-        r = by_table(*cut(gwork[c].reshape(ZL * KB, N)), wout[0], wout[1])
-        planes = by_table(*cut(jnp.concatenate([low, high], axis=0)), sin_r[0], sin_r[1])
+        r = by_table((gwork[c].reshape(ZL * KB, N)), wout[0], wout[1])
+        planes = by_table((jnp.concatenate([low, high], axis=0)), sin_r[0], sin_r[1])
         edge = []
         for t in range(2):
             value = near[c][t]
@@ -469,24 +478,22 @@
                     value = jnp.where((lanes >= first) & (lanes < stop), piece, value)
             piece = rolled(edge[p // 8], 2 * YL - 16 * (p % 8))
             bbuf[c, p] = jnp.where((lanes >= 2 * YL) & (lanes < 2 * YL + 16), piece, value)
-        for d in range(1, NB):
+        for d in PA_ORDER:
             p = peer(pa, d)
-            start(remote(bbuf.at[c, p], mine(brecv, c, pa), bsend_s.at[c, d], brecv_s.at[c, pa], {"pa": p}))
+            remote(bbuf.at[c, p], mine(brecv, c, pa), bsend_s.at[c], brecv_s.at[c], {"pa": p}).start()
         brecv[c, pl.ds(pl.multiple_of(pa * KB, KB), KB), :] = bbuf[c, pa]
 
     def again(c):
-        for d in range(1, NB):
-            p = peer(pa, d)
-            remote(bbuf.at[c, p], mine(brecv, c, p), bsend_s.at[c, d], brecv_s.at[c, p], {"pa": p}).wait_recv()
+        wait_all(bbuf.at[c, 0 : NB - 1], brecv_s.at[c])
         if c == 0:
             need("mc", "bwd")
         x = jnp.concatenate(
             [jnp.transpose(brecv[c, t * LANES : (t + 1) * LANES, :]) for t in range(CW // LANES)], axis=1
         )
-        add = table_by(mc[0], mc[1], x)
+        add = table_by(mc[...], x)
         solve(lambda z: fh[c, z] + add[z * YL : (z + 1) * YL], eloc.at[c], work.at[c])
         u = jnp.concatenate([sines(work[c, z]) for z in range(ZL)], axis=0)
-        part = by_table(*cut(u), bwd[c, 0], bwd[c, 1])
+        part = by_table(u, bwd[c, 0], bwd[c, 1])
         if c == 0:
             out[...] = part
         else:
@@ -501,20 +508,19 @@
     for c in range(NC):
         again(c)
 
-    for copy in copies:
-        copy.wait_send()
-    for c in range(NC):
-        for s, g in enumerate(SOLVERS):
-
-            @pl.when(gz != g)
-            def _():
-                remote(qbuf.at[c, s], qrecv.at[c, gz], qsend_s.at[c, s], qrecv_s.at[c, gz], {"gz": g}).wait_send()
+    wait_all(widths.at[0 : NB - 1], send_s.at[0])
+    for c in range(NC):
+        wait_all(precv.at[c, 0 : NB - 1], psend_s.at[c])
+        wait_all(bbuf.at[c, 0 : NB - 1], bsend_s.at[c])
+
+        @pl.when(jnp.logical_not(is_solver))
+        def _():
+            wait_all(qbuf.at[c], qsend_s.at[c])
 
         @pl.when(is_solver)
         def _():
-            for d in range(1, NB):
-                g = peer(gz, d)
-                remote(rbuf.at[c, g], rrecv.at[c, me_s], rsend_s.at[c, d], rrecv_s.at[c, me_s], {"gz": g}).wait_send()
+            wait_all(qbuf.at[c, 0 : NS - 1], qsend_s.at[c])
+            wait_all(rbuf.at[c, 0 : NB - 1], rsend_s.at[c])
 
 
 def on_device(source, cell_width):
@@ -559,13 +565,11 @@
             v((NB, 8, LANES), F32),
             v((NC, NB, KB, LANES), F32),
             v((NC, CW, LANES), F32),
-            dma((24,)),
-            dma((NC, NB)),
-            dma((NC, NB)),
-            dma((NB,)),
-            dma((NB,)),
+            dma((16,)),
+            dma((1,)),
+            dma((1,)),
         ]
-        + [dma((NC, NB))] * 6,
+        + [dma((NC,))] * 8,
         compiler_params=pltpu.CompilerParams(
             collective_id=0, has_side_effects=True, vmem_limit_bytes=44 * 1024 * 1024
         ),

time: 50.8 us -> 46.2 us (0.909)
  Pallas kernels: 49.7 us -> 45 us
    pallas_call x1, Pallas kernels: 49.7 us -> 45 us  [on_device(): pl.pallas_call(kernel, out_shape=jax.ShapeDtypeStruct((ZL * YL, N), F32),...]
where the time goes in v2:
time: 46.2 us; the launch traced here: 46 us
  Pallas kernels  45 us (97%)
  local copies, waits for them, and re-layouts  1.02 us (2%)
    pallas_call x1, Pallas kernels, on_device(): pl.pallas_call(kernel, out_shape=jax.ShapeDtypeStruct((ZL * YL, N), F32),...  45 us
    unnamed x1, local copies, waits for them, and re-layouts  1.02 us

profile of v2, /device:TPU:1, one launch (start us, length us, event | category | flops | bytes accessed | tf_op | source)
XLA Modules:
  0.0 46.0 jit_solution(17240651020114889931)
XLA Ops:
  0.0 45.0 %poisson.1 = f32[384,768]{1,0:T(8,128)S(1)} custom-call(f32[384,768]{1,0:T(8,128)} %bitcast.3, f32[8]{0:T(128)} %cw.1, bf16[3,2,768,256]{3,2,1,0:T(8,128)(2,1)} %constant.22.clone.fwd_h, bf16[3,2,256,768]{3,2,1,0:T(8,128)(2,1)} %constant.23.clone.bwd_h, bf16[2,768,768]{2,1,0:T(8,128)(2,1)} %constant.24.clone.sin_h, bf16[48,144]{1,0:T(8,128)(2,1)} %constant.25.clone.s48_h, ...), custom_call_target="tpu_custom_call" | custom-call | tf_op jit(solution)/shard_map/poisson/pallas_call | solution.py:534
  45.0 1.0 %copy.15 = f32[8,48,768]{2,1,0:T(8,128)} copy(f32[8,48,768]{2,1,0:T(8,128)S(1)} %bitcast.2) | data formatting | bytes 2359296

commit v3 on v2

--- a/solution.py
+++ b/solution.py
@@ -49,12 +49,12 @@
     s48 = sine(YL, ml, ml)
     hi, lo = split64(s48)
     s48st = np.concatenate([hi, hi, lo], axis=1)
-    mc = np.zeros((ZL * YL, LANES))
-    mc[:YL, :YL] = s48
-    mc[(ZL - 1) * YL :, YL : 2 * YL] = s48
+    mcp = np.zeros((2, ZL * YL, LANES // 2))
+    mcp[0, :YL, :YL] = s48
+    mcp[1, (ZL - 1) * YL :, :YL] = s48
     for z in range(ZL):
-        mc[z * YL : (z + 1) * YL, 2 * YL + 2 * z] = s48[:, 0]
-        mc[z * YL : (z + 1) * YL, 2 * YL + 2 * z + 1] = s48[:, YL - 1]
+        mcp[:, z * YL : (z + 1) * YL, YL + 2 * z] = s48[:, 0]
+        mcp[:, z * YL : (z + 1) * YL, YL + 2 * z + 1] = s48[:, YL - 1]
     own = np.zeros((NB, ZL, 2, N))
     beside = np.zeros((NB, ZL, 2, N))
     for p in range(NB):
@@ -78,13 +78,13 @@
         bwd=np.ascontiguousarray(cos2.reshape(2, NC, CW, N).transpose(1, 0, 2, 3)),
         sin=split64(sin_t),
         s48=s48st,
-        mct=split64(mc.T.copy()).reshape(2 * LANES, ZL * YL),
-        mc=split64(mc).reshape(2 * ZL * YL, LANES),
+        mct=split64(mcp.transpose(0, 2, 1).copy()).transpose(1, 0, 2, 3).reshape(2, LANES, ZL * YL),
+        mc=split64(mcp).transpose(1, 0, 2, 3).reshape(2, 2 * ZL * YL, LANES // 2),
         win=split64(own),
         wout=split64(beside.T.copy()),
         rows=rows,
         lam_s=np.broadcast_to(lam_s[:, None], (YL, CW)).astype(np.float32),
-        lam_k=np.broadcast_to(lam_k[:, None], (N, LANES)).astype(np.float32).reshape(NC * NB, KB, LANES),
+        lam_k=np.broadcast_to(lam_k[:, None], (N, LANES)).astype(np.float32).reshape(NC * 2 * NB, 8, LANES),
     )
 
 
@@ -141,12 +141,14 @@
 def kernel(
     src_h, cw, fwd_h, bwd_h, sin_h, s48_h, mct_h, mc_h, win_h, wout_h, rows_h, lam_s_h, lam_k_h, out,
     src, fwd, bwd, sin_r, s48, mct, mc, win, wout, lam_rows, lam_s, lam_k,
-    s_hi, s_lo, fh, work, eloc, pbuf, precv, wmine, widths, alpha, beta, r_before, r_after,
+    s_st, fh, work, eloc, pbuf, precv, wmine, wother, widths, alpha, beta, r_before, r_after,
     rhy, eg, gwork, qbuf, qrecv, rbuf, rrecv, ks, ku0, ku7, kv0, kv7, kh, kia, kc, hh, ss, bbuf, brecv,
-    load_s, send_s, recv_s, psend_s, precv_s, qsend_s, qrecv_s, rsend_s, rrecv_s, bsend_s, brecv_s,
+    m_own, m_other, xbuf, xrecv,
+    load_s, send_s, recv_s, psend_s, precv_s, qsend_s, qrecv_s, rsend_s, rrecv_s, bsend_s, brecv_s, xsend_s, xrecv_s,
 ):
     pa = lax.axis_index("pa")
     gz = lax.axis_index("gz")
+    core = lax.rem(gz, 2)
 
     def peer(me, d):
         return lax.rem(me + d, NB)
@@ -166,9 +168,10 @@
     load("src", src_h, src)
     load("fwd0", fwd_h.at[0], fwd.at[0])
     load("s48", s48_h, s48)
-    load("mct", mct_h, mct)
+    load("mct", mct_h.at[core], mct)
     for c in range(NC):
-        load("lam_k%d" % c, lam_k_h.at[NB * c + pa], lam_k.at[c])
+        for h in range(2):
+            load("lam_k%d" % (2 * c + h), lam_k_h.at[NB * (2 * c + h) + pa], lam_k.at[c, h])
 
     barrier = pltpu.get_barrier_semaphore()
     for d in range(1, NB):
@@ -177,10 +180,13 @@
 
     for z in range(ZL):
         wmine[z : z + 1, :] = jnp.full((1, LANES), cw[z], F32)
-    w = wmine[...]
-    at = lax.broadcasted_iota(jnp.int32, (ZL, LANES), 0)
-    al_b = 2.0 / ((jnp.where(at == 0, w, pltpu.roll(w, 1, axis=0)) + w) * w)
-    be_b = 2.0 / ((w + jnp.where(at == ZL - 1, w, pltpu.roll(w, ZL - 1, axis=0))) * w)
+    def own_links(w):
+        at = lax.broadcasted_iota(jnp.int32, (ZL, LANES), 0)
+        al = 2.0 / ((jnp.where(at == 0, w, pltpu.roll(w, 1, axis=0)) + w) * w)
+        be = 2.0 / ((w + jnp.where(at == ZL - 1, w, pltpu.roll(w, ZL - 1, axis=0))) * w)
+        return al, be
+
+    al_b, be_b = own_links(wmine[...])
 
     def a_of(z, like):
         return wide(al_b[z : z + 1, :], like)
@@ -216,59 +222,119 @@
     need("rows", "lam_s")
     for c in range(NC):
         factor(eloc.at[c], lam_s[...] + lam_rows[0:1, c * CW : (c + 1) * CW])
-    need("src", "fwd0", "s48")
+    need("src", "s48")
     load("fwd1", fwd_h.at[1], fwd.at[1])
     load("fwd2", fwd_h.at[2], fwd.at[2])
-    s_hi[...], s_lo[...] = cut(src[...])
+    s_st[0 : ZL * YL], s_st[ZL * YL :] = cut(src[...])
 
     def sines(x):
         a, b = cut(x)
         return dot(s48[...], jnp.concatenate([a, b, a], axis=0))
 
+    def rows_of(q):
+        return pl.ds(pl.multiple_of(q * 8, 8), 8)
+
+    def wait_all(ref, sem):
+        pltpu.make_async_copy(ref, ref, sem).wait()
+
+    partner = {"gz": gz + 1 - 2 * core}
+
+    def pair(c):
+        w_o = wother[...]
+        w_m = wmine[...]
+        al_o, be_o = own_links(w_o)
+        like = (YL, CW)
+
+        def by_core(x, y):
+            return jnp.where(core == 0, x, y)
+
+        w_l, w_u = by_core(w_m, w_o), by_core(w_o, w_m)
+        al_l, be_l = by_core(al_b, al_o), by_core(be_b, be_o)
+        al_u, be_u = by_core(al_o, al_b), by_core(be_o, be_b)
+
+        def row(x, z):
+            return wide(x[z : z + 1, :], like)
+
+        link_l = 2.0 / ((w_l[ZL - 1 : ZL] + w_u[0:1]) * w_l[ZL - 1 : ZL])
+        link_u = 2.0 / ((w_l[ZL - 1 : ZL] + w_u[0:1]) * w_u[0:1])
+        more_l = wide(be_l[ZL - 1 : ZL] - link_l, like)
+        more_u = wide(al_u[0:1] - link_u, like)
+        link_l = wide(link_l, like)
+        link_u = wide(link_u, like)
+        lam = lam_s[...] + lam_rows[0:1, c * CW : (c + 1) * CW]
+        g_l = recip(row(al_l, 0) + row(be_l, 0) + lam)
+        for z in range(1, ZL):
+            g_l = recip(row(al_l, z) + row(be_l, z) + lam - row(al_l, z) * row(be_l, z - 1) * g_l)
+        g_u = recip(row(al_u, ZL - 1) + row(be_u, ZL - 1) + lam)
+        for z in range(ZL - 2, -1, -1):
+            g_u = recip(row(al_u, z) + row(be_u, z) + lam - row(be_u, z) * row(al_u, z + 1) * g_u)
+        rest_l = 1.0 - g_l * more_l
+        rest_u = 1.0 - g_u * more_u
+        inv = recip(rest_l * rest_u - g_l * g_u * link_l * link_u)
+        own_l = link_l * link_u * g_u + more_l * rest_u
+        own_u = link_l * link_u * g_l + more_u * rest_l
+        m_own[c] = by_core(own_l, own_u) * inv
+        m_other[c] = by_core(link_l, link_u) * inv
+
+    def alone(c, i):
+        first, last = solve(lambda z: fh[c, z], eloc.at[c], work.at[c])
+        xbuf[i, c] = jnp.where(core == 0, last, first)
+
+    def exchange(c, i):
+        remote(xbuf.at[i, c], xrecv.at[i, c], xsend_s.at[i, c], xrecv_s.at[i, c], partner).start()
+
+    def paired(c, i):
+        wait_all(xrecv.at[i, c], xrecv_s.at[i, c])
+        more = m_own[c] * xbuf[i, c] + m_other[c] * xrecv[i, c]
+        ends_of = {0: jnp.where(core == 0, 0.0, more), ZL - 1: jnp.where(core == 0, more, 0.0)}
+        solve(lambda z: fh[c, z] + ends_of[z] if z in ends_of else fh[c, z], eloc.at[c], work.at[c])
+
     def block(c):
-        f = dot(s_hi[...], fwd[c, 0]) + dot(s_lo[...], fwd[c, 0]) + dot(s_hi[...], fwd[c, 1])
+        need("fwd%d" % c)
+        f = dot(s_st[...], fwd[c, 0])
+        f = f[: ZL * YL] + f[ZL * YL :] + dot(s_st[0 : ZL * YL], fwd[c, 1])
         for z in range(ZL):
             fh[c, z] = sines(f[z * YL : (z + 1) * YL])
+        alone(c, 0)
+
+    def perimeter(c):
+        paired(c, 0)
         if c == 0:
             need("mct")
-        solve(lambda z: fh[c, z], eloc.at[c], work.at[c])
         p = table_by(mct[...], work[c].reshape(ZL * YL, CW))
-        for t in range(CW // LANES):
-            cols = slice(t * LANES, (t + 1) * LANES)
-            pbuf[c, cols, :] = jnp.transpose(p[:, cols])
-
-    def mine(ref, c, q):
-        return ref.at[c, pl.ds(pl.multiple_of(q * KB, KB), KB), :]
-
-    def wait_all(ref, sem):
-        pltpu.make_async_copy(ref, ref, sem).wait()
-
-    def send_perimeter(c):
+        pbuf[c] = jnp.transpose(jnp.concatenate([p[:, :LANES], p[:, LANES:]], axis=0))
         for d in PA_ORDER:
             q = peer(pa, d)
-            remote(mine(pbuf, c, q), precv.at[c, pa], psend_s.at[c], precv_s.at[c], {"pa": q}).start()
-        precv[c, pa] = pbuf[c, pl.ds(pl.multiple_of(pa * KB, KB), KB), :]
-
+            remote(pbuf.at[c, rows_of(q), :], precv.at[c, pa], psend_s.at[c], precv_s.at[c], {"pa": q}).start()
+        precv[c, pa] = pbuf[c, rows_of(pa), :]
+
+    block(0)
+    load("win", win_h, win)
+    load("sin", sin_h, sin_r)
+    load("wout", wout_h, wout)
+    load("mc", mc_h.at[core], mc)
+    load("bwd", bwd_h, bwd)
+    pl.semaphore_wait(barrier, 2 * (NB - 1))
+    remote(wmine, wother, send_s.at[1], recv_s.at[1], partner).start()
+    exchange(0, 0)
+    for d in GZ_ORDER:
+        remote(wmine, widths.at[gz], send_s.at[0], recv_s.at[0], {"gz": peer(gz, d)}).start()
+    widths[gz] = wmine[...]
+    block(1)
+    exchange(1, 0)
+    wait_all(wother, recv_s.at[1])
+    pair(0)
+    perimeter(0)
+    block(2)
+    exchange(2, 0)
+    pair(1)
+    perimeter(1)
+    pair(2)
+    perimeter(2)
+
+    need(*("lam_k%d" % c for c in range(2 * NC)))
     for c in range(NC):
-        if c:
-            need("fwd%d" % c)
-        block(c)
-        if c == 0:
-            load("win", win_h, win)
-            load("sin", sin_h, sin_r)
-            load("wout", wout_h, wout)
-            load("mc", mc_h, mc)
-            load("bwd", bwd_h, bwd)
-            pl.semaphore_wait(barrier, 2 * (NB - 1))
-        send_perimeter(c)
-        if c == 0:
-            for d in GZ_ORDER:
-                remote(wmine, widths.at[gz], send_s.at[0], recv_s.at[0], {"gz": peer(gz, d)}).start()
-            widths[gz] = wmine[...]
-
-    need(*("lam_k%d" % c for c in range(NC)))
-    for c in range(NC):
-        factor(eg.at[c], wide(lam_k[c], (KB, N)) + lam_rows[1:2, :])
+        factor(eg.at[c], wide(lam_k[c].reshape(KB, LANES), (KB, N)) + lam_rows[1:2, :])
 
     wait_all(widths.at[0 : NB - 1], recv_s.at[0])
     w = widths[...].reshape(NB * ZL, LANES)
@@ -297,7 +363,7 @@
     def _():
         rt = lax.div(me_s, CH)
         lt = lax.rem(me_s, CH)
-        lam = jnp.concatenate([lam_k[c, pl.ds(pl.multiple_of(8 * rt, 8), 8), :] for c in range(NC)], axis=0)
+        lam = jnp.concatenate([lam_k[c, rt] for c in range(NC)], axis=0)
         lam = lam + lam_rows[1:2, pl.ds(pl.multiple_of(lt * LANES, LANES), LANES)]
 
         def coefficients(b, carry):
@@ -341,7 +407,7 @@
 
     small = (KB, LANES)
     lanes = lax.broadcasted_iota(jnp.int32, small, 1)
-    odd = lax.rem(lanes, 2) == 1
+    lane8 = lax.broadcasted_iota(jnp.int32, (8, LANES), 1)
     at_z = [lax.div(lax.rem(lanes, 16), 2) == z for z in range(ZL)]
     zero = jnp.zeros(small, F32)
     near = {}
@@ -349,21 +415,24 @@
     def ends(c):
         wait_all(precv.at[c, 0 : NB - 1], precv_s.at[c])
 
-        def gathered(base, t):
-            value = zero
+        tile8 = jnp.zeros((8, LANES), F32)
+        odd = lax.rem(lane8, 2) == 1
+
+        def gathered(h, t):
+            value = tile8
             for p in range(NB):
                 first = YL * p - LANES * t
                 if first + YL <= 0 or first >= LANES:
                     continue
-                piece = rolled(precv[c, p], first - base)
-                value = jnp.where((lanes >= first) & (lanes < first + YL), piece, value)
+                piece = rolled(precv[c, p], first - LANES // 2 * h)
+                value = jnp.where((lane8 >= first) & (lane8 < first + YL), piece, value)
             return value
 
-        def beside(t):
-            value = zero
+        def beside(h, t):
+            value = tile8
             for p in range(8 * t, 8 * t + 8):
-                at_p = lax.div(lanes, 16) == p - 8 * t
-                first = 16 * (p - 8 * t) - 2 * YL
+                at_p = lax.div(lane8, 16) == p - 8 * t
+                first = 16 * (p - 8 * t) - LANES // 2 * h - YL
                 if p > 0:
                     value = jnp.where(at_p & ~odd, rolled(precv[c, p - 1], first - 1), value)
                 if p < NB - 1:
@@ -371,9 +440,9 @@
             return value
 
         planes = jnp.concatenate(
-            [jnp.concatenate([gathered(base, t) for t in range(CH)], axis=1) for base in (0, YL)], axis=0
+            [jnp.concatenate([gathered(h, t) for t in range(CH)], axis=1) for h in range(2)], axis=0
         )
-        near[c] = [beside(t) for t in range(2)]
+        near[c] = [jnp.concatenate([beside(h, t) for h in range(2)], axis=0) for t in range(2)]
         rows = jnp.concatenate(
             [jnp.concatenate([jnp.where(at_z[z], v, 0.0) for v in near[c]], axis=1) for z in range(ZL)], axis=0
         )
@@ -382,7 +451,7 @@
         rhy[c] = by_table(rows, win[0], win[1]).reshape(ZL, KB, N)
         v = by_table(planes, sin_r[0], sin_r[1])
         first, last = solve(lambda z: rhy[c, z], eg.at[c], gwork.at[c])
-        q = (v[0:KB] + first, v[KB : 2 * KB] + last)
+        q = (first + jnp.where(core == 0, v, 0.0), last + jnp.where(core == 0, 0.0, v))
         for s in range(NS):
             rt, lt = divmod(s, CH)
             for i in range(2):
@@ -460,7 +529,7 @@
         if c == 0:
             need("wout")
         r = by_table((gwork[c].reshape(ZL * KB, N)), wout[0], wout[1])
-        planes = by_table((jnp.concatenate([low, high], axis=0)), sin_r[0], sin_r[1])
+        planes = by_table(jnp.where(core == 0, low, high), sin_r[0], sin_r[1])
         edge = []
         for t in range(2):
             value = near[c][t]
@@ -468,30 +537,39 @@
                 value = value + jnp.where(at_z[z], r[z * KB : (z + 1) * KB, t * LANES : (t + 1) * LANES], 0.0)
             edge.append(value)
         for p in range(NB):
-            value = zero
-            for e in range(2):
+            value = jnp.zeros((8, LANES), F32)
+            for h in range(2):
+                part = slice(8 * h, 8 * h + 8)
+                base = h * LANES // 2
                 for t in range(YL * p // LANES, (YL * p + YL - 1) // LANES + 1):
-                    move = YL * e - YL * p
+                    move = base - YL * p
                     first = max(LANES * t, YL * p) + move
                     stop = min(LANES * (t + 1), YL * p + YL) + move
-                    piece = rolled(planes[e * KB : (e + 1) * KB, t * LANES : (t + 1) * LANES], LANES * t + move)
-                    value = jnp.where((lanes >= first) & (lanes < stop), piece, value)
-            piece = rolled(edge[p // 8], 2 * YL - 16 * (p % 8))
-            bbuf[c, p] = jnp.where((lanes >= 2 * YL) & (lanes < 2 * YL + 16), piece, value)
+                    piece = rolled(planes[part, t * LANES : (t + 1) * LANES], LANES * t + move)
+                    value = jnp.where((lane8 >= first) & (lane8 < stop), piece, value)
+                first = base + YL
+                piece = rolled(edge[p // 8][part], first - 16 * (p % 8))
+                value = jnp.where((lane8 >= first) & (lane8 < first + 16), piece, value)
+            bbuf[c, p] = value
         for d in PA_ORDER:
             p = peer(pa, d)
-            remote(bbuf.at[c, p], mine(brecv, c, pa), bsend_s.at[c], brecv_s.at[c], {"pa": p}).start()
-        brecv[c, pl.ds(pl.multiple_of(pa * KB, KB), KB), :] = bbuf[c, pa]
+            remote(bbuf.at[c, p], brecv.at[c, rows_of(pa), :], bsend_s.at[c], brecv_s.at[c], {"pa": p}).start()
+        brecv[c, rows_of(pa), :] = bbuf[c, pa]
 
     def again(c):
         wait_all(bbuf.at[c, 0 : NB - 1], brecv_s.at[c])
         if c == 0:
             need("mc", "bwd")
-        x = jnp.concatenate(
-            [jnp.transpose(brecv[c, t * LANES : (t + 1) * LANES, :]) for t in range(CW // LANES)], axis=1
-        )
-        add = table_by(mc[...], x)
-        solve(lambda z: fh[c, z] + add[z * YL : (z + 1) * YL], eloc.at[c], work.at[c])
+        half = LANES // 2
+        x = jnp.transpose(brecv[c])
+        add = table_by(mc[...], jnp.concatenate([x[:half], x[half:]], axis=1))
+        for z in range(ZL):
+            fh[c, z] = fh[c, z] + add[z * YL : (z + 1) * YL]
+        alone(c, 1)
+        exchange(c, 1)
+
+    def finish(c):
+        paired(c, 1)
         u = jnp.concatenate([sines(work[c, z]) for z in range(ZL)], axis=0)
         part = by_table(u, bwd[c, 0], bwd[c, 1])
         if c == 0:
@@ -505,13 +583,20 @@
         pl.when(is_solver)(functools.partial(chain, c))
     for c in range(NC):
         inner(c)
-    for c in range(NC):
-        again(c)
+    again(0)
+    again(1)
+    finish(0)
+    again(2)
+    finish(1)
+    finish(2)
 
     wait_all(widths.at[0 : NB - 1], send_s.at[0])
+    wait_all(wother, send_s.at[1])
     for c in range(NC):
         wait_all(precv.at[c, 0 : NB - 1], psend_s.at[c])
         wait_all(bbuf.at[c, 0 : NB - 1], bsend_s.at[c])
+        for i in range(2):
+            wait_all(xbuf.at[i, c], xsend_s.at[i, c])
 
         @pl.when(jnp.logical_not(is_solver))
         def _():
@@ -529,7 +614,7 @@
     hbm = pl.BlockSpec(memory_space=pltpu.HBM)
     v = pltpu.VMEM
     dma = pltpu.SemaphoreType.DMA
-    here = [v(x.shape, x.dtype) for x in args[:-1]] + [v((NC, KB, LANES), F32)]
+    here = [v(x.shape[1:] if n in ("mc", "mct") else x.shape, x.dtype) for n, x in zip(TABLES[:-1], args)] + [v((NC, 2, 8, LANES), F32)]
     coef = v((NB, 8 * NC, LANES), F32)
     out = pl.pallas_call(
         kernel,
@@ -539,13 +624,13 @@
         scratch_shapes=[v((ZL * YL, N), F32)]
         + here
         + [
-            v((ZL * YL, N), BF16),
-            v((ZL * YL, N), BF16),
+            v((2 * ZL * YL, N), BF16),
             v((NC, ZL, YL, CW), F32),
             v((NC, ZL, YL, CW), F32),
             v((NC, ZL, YL, CW), F32),
-            v((NC, CW, LANES), F32),
-            v((NC, NB, KB, LANES), F32),
+            v((NC, LANES, LANES), F32),
+            v((NC, NB, 8, LANES), F32),
+            v((ZL, LANES), F32),
             v((ZL, LANES), F32),
             v((NB, ZL, LANES), F32),
         ]
@@ -563,13 +648,18 @@
         + [
             v((NB, 8, LANES), F32),
             v((NB, 8, LANES), F32),
-            v((NC, NB, KB, LANES), F32),
-            v((NC, CW, LANES), F32),
-            dma((16,)),
-            dma((1,)),
-            dma((1,)),
+            v((NC, NB, 8, LANES), F32),
+            v((NC, LANES, LANES), F32),
         ]
-        + [dma((NC,))] * 8,
+        + [v((NC, YL, CW), F32)] * 2
+        + [v((2, NC, YL, CW), F32)] * 2
+        + [
+            dma((24,)),
+            dma((2,)),
+            dma((2,)),
+        ]
+        + [dma((NC,))] * 8
+        + [dma((2, NC))] * 2,
         compiler_params=pltpu.CompilerParams(
             collective_id=0, has_side_effects=True, vmem_limit_bytes=44 * 1024 * 1024
         ),

time: 46.2 us -> 44.5 us (0.963)
  Pallas kernels: 45 us -> 43.4 us
    pallas_call x1, Pallas kernels: 45 us -> 43.4 us  [on_device(): pl.pallas_call(kernel, out_shape=jax.ShapeDtypeStruct((ZL * YL, N), F32),...]
where the time goes in v3:
time: 44.5 us; the launch traced here: 44.4 us
  Pallas kernels  43.4 us (98%)
  local copies, waits for them, and re-layouts  1.02 us (2%)
    pallas_call x1, Pallas kernels, on_device(): pl.pallas_call(kernel, out_shape=jax.ShapeDtypeStruct((ZL * YL, N), F32),...  43.4 us
    unnamed x1, local copies, waits for them, and re-layouts  1.02 us

profile of v3, /device:TPU:1, one launch (start us, length us, event | category | flops | bytes accessed | tf_op | source)
XLA Modules:
  0.0 44.4 jit_solution(18043269877791356646)
XLA Ops:
  0.0 43.4 %poisson.1 = f32[384,768]{1,0:T(8,128)S(1)} custom-call(f32[384,768]{1,0:T(8,128)} %bitcast.3, f32[8]{0:T(128)} %cw.1, bf16[3,2,768,256]{3,2,1,0:T(8,128)(2,1)} %constant.22.clone.fwd_h, bf16[3,2,256,768]{3,2,1,0:T(8,128)(2,1)} %constant.23.clone.bwd_h, bf16[2,768,768]{2,1,0:T(8,128)(2,1)} %constant.24.clone.sin_h, bf16[48,144]{1,0:T(8,128)(2,1)} %constant.25.clone.s48_h, ...), custom_call_target="tpu_custom_call" | custom-call | tf_op jit(solution)/shard_map/poisson/pallas_call | solution.py:619
  43.4 1.0 %copy.15 = f32[8,48,768]{2,1,0:T(8,128)} copy(f32[8,48,768]{2,1,0:T(8,128)S(1)} %bitcast.2) | data formatting | bytes 2359296

commit v4 on v3

--- a/solution.py
+++ b/solution.py
@@ -75,11 +75,11 @@
     cos2 = split64(cos_t)
     return dict(
         fwd=np.ascontiguousarray(cos2.reshape(2, NC, CW, N).transpose(1, 0, 3, 2)),
-        bwd=np.ascontiguousarray(cos2.reshape(2, NC, CW, N).transpose(1, 0, 2, 3)),
+        bwd=cos2,
         sin=split64(sin_t),
         s48=s48st,
         mct=split64(mcp.transpose(0, 2, 1).copy()).transpose(1, 0, 2, 3).reshape(2, LANES, ZL * YL),
-        mc=split64(mcp).transpose(1, 0, 2, 3).reshape(2, 2 * ZL * YL, LANES // 2),
+        mc=np.concatenate([split64(mcp)[i] for i in (0, 0, 1)], axis=2),
         win=split64(own),
         wout=split64(beside.T.copy()),
         rows=rows,
@@ -105,6 +105,10 @@
     m = x.shape[0]
     r = dot(jnp.concatenate([a, b], axis=0), hi)
     return r[:m] + r[m:] + dot(a, lo)
+
+
+def stacked(a, b, hi, lo):
+    return dot(jnp.concatenate([a, b, a], axis=1), jnp.concatenate([hi, hi, lo], axis=0))
 
 
 def table_by(t, x):
@@ -562,17 +566,22 @@
             need("mc", "bwd")
         half = LANES // 2
         x = jnp.transpose(brecv[c])
-        add = table_by(mc[...], jnp.concatenate([x[:half], x[half:]], axis=1))
+        a, b = cut(jnp.concatenate([x[:half], x[half:]], axis=1))
+        add = dot(mc[...], jnp.concatenate([a, b, a], axis=0))
         for z in range(ZL):
             fh[c, z] = fh[c, z] + add[z * YL : (z + 1) * YL]
         alone(c, 1)
         exchange(c, 1)
 
-    def finish(c):
-        paired(c, 1)
-        u = jnp.concatenate([sines(work[c, z]) for z in range(ZL)], axis=0)
-        part = by_table(u, bwd[c, 0], bwd[c, 1])
-        if c == 0:
+    def finish(*batches):
+        us = []
+        for c in batches:
+            paired(c, 1)
+            us.append(jnp.concatenate([sines(work[c, z]) for z in range(ZL)], axis=0))
+        u = jnp.concatenate(us, axis=1)
+        rows = slice(batches[0] * CW, (batches[-1] + 1) * CW)
+        part = stacked(*cut(u), bwd[0, rows], bwd[1, rows])
+        if batches[0] == 0:
             out[...] = part
         else:
             out[...] += part
@@ -584,8 +593,8 @@
     for c in range(NC):
         inner(c)
     again(0)
+    finish(0)
     again(1)
-    finish(0)
     again(2)
     finish(1)
     finish(2)

time: 44.5 us -> 43.8 us (0.984)
  Pallas kernels: 43.4 us -> 42.7 us
    pallas_call x1, Pallas kernels: 43.4 us -> 42.7 us  [on_device(): pl.pallas_call(kernel, out_shape=jax.ShapeDtypeStruct((ZL * YL, N), F32),...]
where the time goes in v4:
time: 43.8 us; the launch traced here: 43.7 us
  Pallas kernels  42.7 us (97%)
  local copies, waits for them, and re-layouts  1.02 us (2%)
    pallas_call x1, Pallas kernels, on_device(): pl.pallas_call(kernel, out_shape=jax.ShapeDtypeStruct((ZL * YL, N), F32),...  42.7 us
    unnamed x1, local copies, waits for them, and re-layouts  1.02 us

profile of v4, /device:TPU:1, one launch (start us, length us, event | category | flops | bytes accessed | tf_op | source)
XLA Modules:
  0.0 43.7 jit_solution(7957749544081716472)
XLA Ops:
  0.0 42.7 %poisson.1 = f32[384,768]{1,0:T(8,128)S(1)} custom-call(f32[384,768]{1,0:T(8,128)} %bitcast.3, f32[8]{0:T(128)} %cw.1, bf16[3,2,768,256]{3,2,1,0:T(8,128)(2,1)} %constant.22.clone.fwd_h, bf16[2,768,768]{2,1,0:T(8,128)(2,1)} %constant.23.clone.bwd_h, bf16[2,768,768]{2,1,0:T(8,128)(2,1)} %constant.24.clone.sin_h, bf16[48,144]{1,0:T(8,128)(2,1)} %constant.25.clone.s48_h, ...), custom_call_target="tpu_custom_call" | custom-call | tf_op jit(solution)/shard_map/poisson/pallas_call | solution.py:628
  42.7 1.0 %copy.15 = f32[8,48,768]{2,1,0:T(8,128)} copy(f32[8,48,768]{2,1,0:T(8,128)S(1)} %bitcast.2) | data formatting | bytes 2359296

commit v5 on v4

--- a/solution.py
+++ b/solution.py
@@ -107,10 +107,6 @@
     return r[:m] + r[m:] + dot(a, lo)
 
 
-def stacked(a, b, hi, lo):
-    return dot(jnp.concatenate([a, b, a], axis=1), jnp.concatenate([hi, hi, lo], axis=0))
-
-
 def table_by(t, x):
     a, b = cut(x)
     m = t.shape[0] // 2
@@ -580,7 +576,7 @@
             us.append(jnp.concatenate([sines(work[c, z]) for z in range(ZL)], axis=0))
         u = jnp.concatenate(us, axis=1)
         rows = slice(batches[0] * CW, (batches[-1] + 1) * CW)
-        part = stacked(*cut(u), bwd[0, rows], bwd[1, rows])
+        part = by_table(u, bwd[0, rows], bwd[1, rows])
         if batches[0] == 0:
             out[...] = part
         else:

time: 43.8 us -> 43.7 us (level)
  no operation moved by 1% of the time
where the time goes in v5:
time: 43.7 us; the launch traced here: 43.6 us
  Pallas kernels  42.6 us (97%)
  local copies, waits for them, and re-layouts  1.02 us (2%)
    pallas_call x1, Pallas kernels, on_device(): pl.pallas_call(kernel, out_shape=jax.ShapeDtypeStruct((ZL * YL, N), F32),...  42.6 us
    unnamed x1, local copies, waits for them, and re-layouts  1.02 us

profile of v5, /device:TPU:1, one launch (start us, length us, event | category | flops | bytes accessed | tf_op | source)
XLA Modules:
  0.0 43.6 jit_solution(9380780923346350417)
XLA Ops:
  0.0 42.6 %poisson.1 = f32[384,768]{1,0:T(8,128)S(1)} custom-call(f32[384,768]{1,0:T(8,128)} %bitcast.3, f32[8]{0:T(128)} %cw.1, bf16[3,2,768,256]{3,2,1,0:T(8,128)(2,1)} %constant.22.clone.fwd_h, bf16[2,768,768]{2,1,0:T(8,128)(2,1)} %constant.23.clone.bwd_h, bf16[2,768,768]{2,1,0:T(8,128)(2,1)} %constant.24.clone.sin_h, bf16[48,144]{1,0:T(8,128)(2,1)} %constant.25.clone.s48_h, ...), custom_call_target="tpu_custom_call" | custom-call | tf_op jit(solution)/shard_map/poisson/pallas_call | solution.py:624
  42.6 1.0 %copy.15 = f32[8,48,768]{2,1,0:T(8,128)} copy(f32[8,48,768]{2,1,0:T(8,128)S(1)} %bitcast.2) | data formatting | bytes 2359296
